TPU v7x, 32 devices: a 4x4x1 block of a 4x4x8 slice. The times are simulated.
32 devices in a mesh: data: 1 (over z), tp: 4 (over y), ep: 8 (over x, core).
Axes of the slice: x: 4, y: 4, z: 1, core: 2. Of those that a mesh axis runs over, the one named last changes fastest.
The devices are a block of a 4x4x8 slice.
Arguments:
- tokens_a: bfloat16 [8192, 1536], P(('data', 'ep', 'tp'))
- tokens_b: bfloat16 [8192, 1536], P(('data', 'ep', 'tp'))
- experts_a: int32 [8192, 6], P(('data', 'ep', 'tp'))
- experts_b: int32 [8192, 6], P(('data', 'ep', 'tp'))
- gates_a: float32 [8192, 6], P(('data', 'ep', 'tp'))
- gates_b: float32 [8192, 6], P(('data', 'ep', 'tp'))
- slots_a: int32 [8192, 6], P(('data', 'ep', 'tp'))
- slots_b: int32 [8192, 6], P(('data', 'ep', 'tp'))
- shared_w1: bfloat16 [1536, 1024], P(None, 'tp')
- shared_w3: bfloat16 [1536, 1024], P(None, 'tp')
- shared_w2: bfloat16 [1024, 1536], P('tp')
- routed_w1: bfloat16 [64, 1536, 512], P('ep')
- routed_w3: bfloat16 [64, 1536, 512], P('ep')
- routed_w2: bfloat16 [64, 512, 1536], P('ep')
Outputs:
- output 1: bfloat16 [8192, 1536], P(('data', 'ep', 'tp'))
- output 2: bfloat16 [8192, 1536], P(('data', 'ep', 'tp'))
All inputs are finite; a program needn't handle non-finite values.
Results may differ from a plain program's by a relative error of at most 0.00607059.
Values are sent between devices in bfloat16 or wider.
A program may use at most 768 MiB of HBM per device.

v0:
```python
import jax
import jax.numpy as jnp
from jax import lax
from jax.sharding import PartitionSpec as P


def capacity_rows(tok_local, top_k, num_experts):
    return max(4, (2 * tok_local * top_k) // num_experts)


def swiglu_rows(rows, w_in, w_gate, w_out):
    proj_in = jnp.dot(rows, w_in, preferred_element_type=jnp.float32)
    proj_gate = jnp.dot(rows, w_gate, preferred_element_type=jnp.float32)
    hidden = (jax.nn.silu(proj_in) * proj_gate).astype(jnp.bfloat16)
    return jnp.dot(hidden, w_out, preferred_element_type=jnp.float32)


def solution(mesh):
    ep_size = mesh.shape['ep']
    tok_spec = P(('data', 'ep', 'tp'), None)
    in_specs = (tok_spec,) * 8 + (P(None, 'tp'), P(None, 'tp'), P('tp', None), P('ep', None, None), P('ep', None, None), P('ep', None, None))

    def shared_path(x_local, shared_w1, shared_w3, shared_w2):
        gathered = lax.all_gather(x_local, 'tp', axis=0, tiled=True)
        partial_sum = swiglu_rows(gathered, shared_w1, shared_w3, shared_w2)
        return lax.psum_scatter(partial_sum, 'tp', scatter_dimension=0, tiled=True)

    def routed_path(x_local, expert_ids, gate_vals, slot_ids, routed_w1, routed_w3, routed_w2):
        tok_local, top_k = expert_ids.shape
        local_experts, model_dim, expert_ff = routed_w1.shape
        cap_rows = capacity_rows(tok_local, top_k, local_experts * ep_size)
        num_rows = local_experts * ep_size * cap_rows
        dest_rank = expert_ids // local_experts
        local_id = expert_ids % local_experts
        keep_mask = slot_ids >= 0
        row_ids = jnp.where(keep_mask, (local_id * ep_size + dest_rank) * cap_rows + slot_ids, -1)
        place_mat = jnp.any(row_ids[:, :, None] == jnp.arange(num_rows)[None, None, :], axis=1).astype(jnp.bfloat16)
        send_rows = jnp.einsum('tr,td->rd', place_mat, x_local, preferred_element_type=jnp.float32).astype(jnp.bfloat16)
        recv_rows = lax.all_to_all(send_rows.reshape(local_experts, ep_size, cap_rows, model_dim), 'ep', 1, 1, tiled=True)
        recv_rows = recv_rows.reshape(local_experts, ep_size * cap_rows, model_dim)
        proj_in = jnp.einsum('erd,edf->erf', recv_rows, routed_w1, preferred_element_type=jnp.float32)
        proj_gate = jnp.einsum('erd,edf->erf', recv_rows, routed_w3, preferred_element_type=jnp.float32)
        hidden = (jax.nn.silu(proj_in) * proj_gate).astype(jnp.bfloat16)
        expert_out = jnp.einsum('erf,efd->erd', hidden, routed_w2, preferred_element_type=jnp.float32).astype(jnp.bfloat16)
        back_rows = lax.all_to_all(expert_out.reshape(local_experts, ep_size, cap_rows, model_dim), 'ep', 1, 1, tiled=True)
        picked = jnp.take(back_rows.reshape(num_rows, model_dim), jnp.maximum(row_ids, 0), axis=0)
        weights = jnp.where(keep_mask, gate_vals, 0.0)
        return jnp.sum(picked.astype(jnp.float32) * weights[:, :, None], axis=1)

    def layer_local(tokens_a, tokens_b, experts_a, experts_b, gates_a, gates_b, slots_a, slots_b, shared_w1, shared_w3, shared_w2, routed_w1, routed_w3, routed_w2):
        def one_microbatch(x_local, expert_ids, gate_vals, slot_ids):
            shared_out = shared_path(x_local, shared_w1, shared_w3, shared_w2)
            routed_out = routed_path(x_local, expert_ids, gate_vals, slot_ids, routed_w1, routed_w3, routed_w2)
            return (x_local.astype(jnp.float32) + shared_out + routed_out).astype(jnp.bfloat16)
        out_a = one_microbatch(tokens_a, experts_a, gates_a, slots_a)
        out_b = one_microbatch(tokens_b, experts_b, gates_b, slots_b)
        return (out_a, out_b)

    return jax.shard_map(layer_local, mesh=mesh, in_specs=in_specs, out_specs=(tok_spec, tok_spec), check_vma=False)
```

profile of v0, /device:TPU:97, one launch (start us, length us, event | category | flops | bytes accessed | tf_op | source)
XLA Modules:
  0.0 534.6 jit_solution(252582416784108533)
XLA Ops:
  7.2 0.0 copy-start
  7.2 0.1 all-gather.5.cloned.1.call-start
  7.3 0.7 all-gather.5.cloned.1.call-update
  8.0 0.7 broadcast_compare_fusion
  8.7 4.2 fusion.1
  12.9 6.3 %convolution_convert_fusion = bf16[3072,1536]{1,0:T(8,128)(2,1)} fusion(pred[256,3072]{1,0:T(8,128)(4,1)S(1)} %fusion.1, bf16[256,1536]{1,0:T(8,128)(2,1)} %param.17), kind=kOutput, calls=%fused_computation.8 | convolution fusion | flops 2420637696 | bytes 11010048 | tf_op jit(solution)/shard_map/tr,td->rd/dot_general | solution.py:38
  19.2 8.2 %copy.54 = bf16[8,8,48,1536]{3,2,0,1:T(8,128)(2,1)} copy(bf16[8,8,48,1536]{3,2,1,0:T(8,128)(2,1)} %bitcast.34) | data formatting | bytes 18874368 | tf_op jit(solution)/shard_map/reshape | solution.py:39
  27.4 7.1 %all-to-all-start.2 = ((bf16[8,8,48,1536]{3,2,0,1:T(8,128)(2,1)}), bf16[8,8,48,1536]{3,2,0,1:T(8,128)(2,1)}, u32[]{:S(2)}, u32[]{:S(2)}) async-start(bf16[8,8,48,1536]{3,2,0,1:T(8,128)(2,1)} %copy.54), calls=%async_computation.4 | async-start | bytes 18874368 | tf_op jit(solution)/shard_map/all_to_all | solution.py:39
  34.5 0.0 all-gather.3.cloned.1.call-start
  34.5 0.8 all-gather.3.cloned.1.call-update
  35.3 0.6 reduce-scatter.5.cloned.1.call-start
  35.9 14.1 %all-gather.5.cloned.1.call-done = bf16[1024,1536]{1,0:T(8,128)(2,1)} async-done(((bf16[256,1536]{1,0:T(8,128)(2,1)}), bf16[1024,1536]{1,0:T(8,128)(2,1)}) %all-gather.5.cloned.1.call-update) | async-done | bytes 3145744 | tf_op jit(solution)/shard_map/all_gather | solution.py:24
  50.0 0.0 copy-done.12
  50.0 2.9 fusion.50
  52.9 0.0 copy-done
  52.9 0.0 copy-done.6
  52.9 0.0 copy-start.8
  52.9 0.0 copy-start.11
  52.9 7.7 %fusion.10 = f32[1024,1536]{1,0:T(8,128)} fusion(bf16[256,1536]{1,0:T(8,128)(2,1)S(1)} %copy-done, bf16[1024,1536]{1,0:T(8,128)(2,1)} %all-gather.5.cloned.1.call-done, bf16[1536,256]{1,0:T(8,128)(2,1)S(1)} %copy-done.6, f32[1024,256]{1,0:T(8,128)S(1)} %fusion.50), kind=kOutput, calls=%fused_computation.24 | convolution fusion | flops 1612185600 | bytes 12058624 | tf_op jit(solution)/shard_map/dot_general | solution.py:15
  60.7 0.1 reduce-scatter.5.cloned.1.call-update
  60.7 0.0 copy-done.8
  60.8 0.0 copy-done.11
  60.8 4.2 fusion
  65.0 5.1 convolution_convert_fusion.1
  70.2 8.2 %copy.47 = bf16[8,8,48,1536]{3,2,0,1:T(8,128)(2,1)} copy(bf16[8,8,48,1536]{3,2,1,0:T(8,128)(2,1)} %bitcast.35) | data formatting | bytes 18874368 | tf_op jit(solution)/shard_map/reshape | solution.py:39
  78.4 61.0 %all-to-all-done.2 = bf16[8,8,48,1536]{3,2,0,1:T(8,128)(2,1)} async-done(((bf16[8,8,48,1536]{3,2,0,1:T(8,128)(2,1)}), bf16[8,8,48,1536]{3,2,0,1:T(8,128)(2,1)}, u32[]{:S(2)}, u32[]{:S(2)}) %all-to-all-start.2) | async-done | bytes 9437216 | tf_op jit(solution)/shard_map/all_to_all | solution.py:39
  139.4 6.3 %all-to-all-start = ((bf16[8,8,48,1536]{3,2,0,1:T(8,128)(2,1)}), bf16[8,8,48,1536]{3,2,0,1:T(8,128)(2,1)}, u32[]{:S(2)}, u32[]{:S(2)}) async-start(bf16[8,8,48,1536]{3,2,0,1:T(8,128)(2,1)} %copy.47), calls=%async_computation.1 | async-start | bytes 18874368 | tf_op jit(solution)/shard_map/all_to_all | solution.py:39
  145.7 8.3 %copy.55 = bf16[8,8,48,1536]{3,2,1,0:T(8,128)(2,1)} copy(bf16[8,8,48,1536]{3,2,0,1:T(8,128)(2,1)} %all-to-all-done.2) | data formatting | bytes 18874368 | tf_op jit(solution)/shard_map/all_to_all | solution.py:39
  154.0 12.9 %fusion.51 = f32[8,384,512]{2,1,0:T(8,128)} fusion(bf16[8,384,1536]{2,1,0:T(8,128)(2,1)} %bitcast.36, bf16[8,1536,512]{2,1,0:T(8,128)(2,1)} %param.27), kind=kOutput, calls=%fused_computation.85 | convolution fusion | flops 4831838208 | bytes 28311552 | tf_op jit(solution)/shard_map/erd,edf->erf/dot_general | solution.py:41
  166.9 26.7 %convolution_convert_fusion.2 = bf16[8,384,1536]{2,1,0:T(8,128)(2,1)} fusion(bf16[8,512,1536]{2,1,0:T(8,128)(2,1)} %param.29, f32[8,384,512]{2,1,0:T(8,128)} %fusion.51, bf16[8,384,1536]{2,1,0:T(8,128)(2,1)} %bitcast.37, bf16[8,1536,512]{2,1,0:T(8,128)(2,1)} %param.28), kind=kOutput, calls=%fused_computation.10 | convolution fusion | flops 9677832192 | bytes 50331648 | tf_op jit(solution)/shard_map/erf,efd->erd/dot_general | solution.py:44
  193.7 8.3 %copy.56 = bf16[8,8,48,1536]{3,2,0,1:T(8,128)(2,1)} copy(bf16[8,8,48,1536]{3,2,1,0:T(8,128)(2,1)} %bitcast.38) | data formatting | bytes 18874368 | tf_op jit(solution)/shard_map/reshape | solution.py:45
  201.9 48.5 %all-to-all-done = bf16[8,8,48,1536]{3,2,0,1:T(8,128)(2,1)} async-done(((bf16[8,8,48,1536]{3,2,0,1:T(8,128)(2,1)}), bf16[8,8,48,1536]{3,2,0,1:T(8,128)(2,1)}, u32[]{:S(2)}, u32[]{:S(2)}) %all-to-all-start) | async-done | bytes 9437216 | tf_op jit(solution)/shard_map/all_to_all | solution.py:39
  250.4 6.0 %all-to-all-start.3 = ((bf16[8,8,48,1536]{3,2,0,1:T(8,128)(2,1)}), bf16[8,8,48,1536]{3,2,0,1:T(8,128)(2,1)}, u32[]{:S(2)}, u32[]{:S(2)}) async-start(bf16[8,8,48,1536]{3,2,0,1:T(8,128)(2,1)} %copy.56), calls=%async_computation.5 | async-start | bytes 18874368 | tf_op jit(solution)/shard_map/all_to_all | solution.py:45
  256.4 0.2 reduce-scatter.3.cloned.1.call-start
  256.7 0.0 all-gather.3.cloned.1.call-done
  256.7 2.9 fusion.48
  259.6 7.8 %fusion.11 = f32[1024,1536]{1,0:T(8,128)} fusion(bf16[256,1536]{1,0:T(8,128)(2,1)S(1)} %copy-done, bf16[1024,1536]{1,0:T(8,128)(2,1)} %all-gather.3.cloned.1.call-done, bf16[1536,256]{1,0:T(8,128)(2,1)S(1)} %copy-done.6, f32[1024,256]{1,0:T(8,128)S(1)} %fusion.48), kind=kOutput, calls=%fused_computation.25 | convolution fusion | flops 1612185600 | bytes 12058624 | tf_op jit(solution)/shard_map/dot_general | solution.py:15
  267.3 0.1 reduce-scatter.3.cloned.1.call-update
  267.4 8.2 %copy.48 = bf16[8,8,48,1536]{3,2,1,0:T(8,128)(2,1)} copy(bf16[8,8,48,1536]{3,2,0,1:T(8,128)(2,1)} %all-to-all-done) | data formatting | bytes 18874368 | tf_op jit(solution)/shard_map/all_to_all | solution.py:39
  275.6 13.0 %fusion.49 = f32[8,384,512]{2,1,0:T(8,128)} fusion(bf16[8,384,1536]{2,1,0:T(8,128)(2,1)} %bitcast.39, bf16[8,1536,512]{2,1,0:T(8,128)(2,1)} %param.27), kind=kOutput, calls=%fused_computation.83 | convolution fusion | flops 4831838208 | bytes 28311552 | tf_op jit(solution)/shard_map/erd,edf->erf/dot_general | solution.py:41
  288.6 26.8 %convolution_convert_fusion.3 = bf16[8,384,1536]{2,1,0:T(8,128)(2,1)} fusion(bf16[8,512,1536]{2,1,0:T(8,128)(2,1)} %param.29, f32[8,384,512]{2,1,0:T(8,128)} %fusion.49, bf16[8,384,1536]{2,1,0:T(8,128)(2,1)} %bitcast.40, bf16[8,1536,512]{2,1,0:T(8,128)(2,1)} %param.28), kind=kOutput, calls=%fused_computation.11 | convolution fusion | flops 9677832192 | bytes 50331648 | tf_op jit(solution)/shard_map/erf,efd->erd/dot_general | solution.py:44
  315.4 8.2 %copy.49 = bf16[8,8,48,1536]{3,2,0,1:T(8,128)(2,1)} copy(bf16[8,8,48,1536]{3,2,1,0:T(8,128)(2,1)} %bitcast.41) | data formatting | bytes 18874368 | tf_op jit(solution)/shard_map/reshape | solution.py:45
  323.6 37.7 %all-to-all-done.3 = bf16[8,8,48,1536]{3,2,0,1:T(8,128)(2,1)} async-done(((bf16[8,8,48,1536]{3,2,0,1:T(8,128)(2,1)}), bf16[8,8,48,1536]{3,2,0,1:T(8,128)(2,1)}, u32[]{:S(2)}, u32[]{:S(2)}) %all-to-all-start.3) | async-done | bytes 9437216 | tf_op jit(solution)/shard_map/all_to_all | solution.py:45
  361.3 6.4 %all-to-all-start.1 = ((bf16[8,8,48,1536]{3,2,0,1:T(8,128)(2,1)}), bf16[8,8,48,1536]{3,2,0,1:T(8,128)(2,1)}, u32[]{:S(2)}, u32[]{:S(2)}) async-start(bf16[8,8,48,1536]{3,2,0,1:T(8,128)(2,1)} %copy.49), calls=%async_computation.2 | async-start | bytes 18874368 | tf_op jit(solution)/shard_map/all_to_all | solution.py:45
  367.7 0.1 copy.58
  367.9 0.1 reshape.69
  368.0 0.2 copy.53
  368.2 0.1 copy.59
  368.4 0.1 copy.51
  368.5 0.1 reshape.65
  368.7 0.2 copy.46
  368.9 0.1 copy.52
  369.0 8.2 %copy.57 = bf16[8,8,48,1536]{3,2,1,0:T(8,128)(2,1)} copy(bf16[8,8,48,1536]{3,2,0,1:T(8,128)(2,1)} %all-to-all-done.3) | data formatting | bytes 18874368 | tf_op jit(solution)/shard_map/all_to_all | solution.py:45
  377.2 15.3 %gather_fusion.1 = bf16[1536,1536]{1,0:T(8,128)(2,1)} fusion(bf16[3072,1536]{1,0:T(8,128)(2,1)} %bitcast.32, s32[2048]{0:T(1024)S(1)} %pad_clamp_fusion), kind=kCustom, calls=%fused_computation.1.clone | custom fusion | bytes 9443328 | tf_op jit(solution)/shard_map/jit(_take)/gather | solution.py:46
  392.5 8.3 %reshape.72 = bf16[256,6,1536]{2,1,0:T(8,128)(2,1)} reshape(bf16[1536,1536]{1,0:T(8,128)(2,1)} %gather_fusion.1) | data formatting | bytes 9437184 | tf_op jit(solution)/shard_map/jit(_take)/gather | solution.py:46
  400.8 71.6 %all-to-all-done.1 = bf16[8,8,48,1536]{3,2,0,1:T(8,128)(2,1)} async-done(((bf16[8,8,48,1536]{3,2,0,1:T(8,128)(2,1)}), bf16[8,8,48,1536]{3,2,0,1:T(8,128)(2,1)}, u32[]{:S(2)}, u32[]{:S(2)}) %all-to-all-start.1) | async-done | bytes 9437216 | tf_op jit(solution)/shard_map/all_to_all | solution.py:45
  472.4 8.3 %copy.50 = bf16[8,8,48,1536]{3,2,1,0:T(8,128)(2,1)} copy(bf16[8,8,48,1536]{3,2,0,1:T(8,128)(2,1)} %all-to-all-done.1) | data formatting | bytes 18874368 | tf_op jit(solution)/shard_map/all_to_all | solution.py:45
  480.7 15.3 %gather_fusion = bf16[1536,1536]{1,0:T(8,128)(2,1)} fusion(bf16[3072,1536]{1,0:T(8,128)(2,1)} %bitcast.33, s32[2048]{0:T(1024)S(1)} %pad_clamp_fusion.1), kind=kCustom, calls=%fused_computation.clone | custom fusion | bytes 9443328 | tf_op jit(solution)/shard_map/jit(_take)/gather | solution.py:46
  495.9 8.3 %reshape.68 = bf16[256,6,1536]{2,1,0:T(8,128)(2,1)} reshape(bf16[1536,1536]{1,0:T(8,128)(2,1)} %gather_fusion) | data formatting | bytes 9437184 | tf_op jit(solution)/shard_map/jit(_take)/gather | solution.py:46
  504.3 9.3 %multiply_reduce_fusion = f32[256,1536]{1,0:T(8,128)} fusion(bf16[256,6,1536]{2,1,0:T(8,128)(2,1)} %reshape.72, f32[256,6]{1,0:T(8,128)S(1)} %copy.59, pred[256,6]{1,0:T(8,128)(4,1)S(1)} %copy.53), kind=kLoop, calls=%fused_computation.6 | loop fusion | flops 9043968 | bytes 6299136 | tf_op jit(solution)/shard_map/reduce_sum | solution.py:48
  513.6 0.0 copy-done.2
  513.6 7.7 %multiply_reduce_fusion.1 = f32[256,1536]{1,0:T(8,128)} fusion(bf16[256,6,1536]{2,1,0:T(8,128)(2,1)S(1)} %copy-done.2, f32[256,6]{1,0:T(8,128)S(1)} %copy.52, pred[256,6]{1,0:T(8,128)(4,1)S(1)} %copy.46), kind=kLoop, calls=%fused_computation.7 | loop fusion | flops 9043968 | bytes 6299136 | tf_op jit(solution)/shard_map/reduce_sum | solution.py:48
  521.3 3.1 add_convert_fusion
  524.4 3.1 add_convert_fusion.1
  (26 shorter events, 0.1 us)
Async XLA Ops:
  7.2 45.7 %copy-start = (bf16[256,1536]{1,0:T(8,128)(2,1)S(1)}, bf16[256,1536]{1,0:T(8,128)(2,1)}, u32[]{:S(2)}) copy-start(bf16[256,1536]{1,0:T(8,128)(2,1)} %param.26) | copy-start | bytes 2359300
  7.2 42.8 %all-gather.5.cloned.1.call-start = ((), (), s32[]{:S(2)}) async-start(), calls=%async_computation.8 | async-start | bytes 3932160 | tf_op jit(solution)/shard_map/all_gather | solution.py:24
  27.4 22.6 %copy-start.12 = (bf16[1536,256]{1,0:T(8,128)(2,1)S(1)}, bf16[1536,256]{1,0:T(8,128)(2,1)}, u32[]{:S(2)}) copy-start(bf16[1536,256]{1,0:T(8,128)(2,1)} %param.24) | copy-start | bytes 2359300
  27.4 112.0 %all-to-all-start.2 = ((bf16[8,8,48,1536]{3,2,0,1:T(8,128)(2,1)}), bf16[8,8,48,1536]{3,2,0,1:T(8,128)(2,1)}, u32[]{:S(2)}, u32[]{:S(2)}) async-start(bf16[8,8,48,1536]{3,2,0,1:T(8,128)(2,1)} %copy.54), calls=%async_computation.4 | async-start | bytes 18874368 | tf_op jit(solution)/shard_map/all_to_all | solution.py:39
  34.5 18.4 %copy-start.6 = (bf16[1536,256]{1,0:T(8,128)(2,1)S(1)}, bf16[1536,256]{1,0:T(8,128)(2,1)}, u32[]{:S(2)}) copy-start(bf16[1536,256]{1,0:T(8,128)(2,1)} %param.25) | copy-start | bytes 2359300
  34.5 222.2 %all-gather.3.cloned.1.call-start = ((), (), s32[]{:S(2)}) async-start(), calls=%async_computation.6 | async-start | bytes 3932160 | tf_op jit(solution)/shard_map/all_gather | solution.py:24
  35.3 486.0 %reduce-scatter.5.cloned.1.call-start = ((), (), s32[]{:S(2)}) async-start(), calls=%async_computation.9 | async-start | bytes 7864320 | tf_op jit(solution)/shard_map/reduce_scatter | solution.py:26
  52.9 7.8 %copy-start.8 = (s32[256,6]{0,1:T(8,128)S(1)}, s32[256,6]{0,1:T(8,128)}, u32[]{:S(2)}) copy-start(s32[256,6]{0,1:T(8,128)} %param.22) | copy-start | bytes 18436
  52.9 7.8 %copy-start.11 = (s32[256,6]{0,1:T(8,128)S(1)}, s32[256,6]{0,1:T(8,128)}, u32[]{:S(2)}) copy-start(s32[256,6]{0,1:T(8,128)} %param.18) | copy-start | bytes 18436
  60.7 4.3 copy-start.4
  139.4 111.1 %all-to-all-start = ((bf16[8,8,48,1536]{3,2,0,1:T(8,128)(2,1)}), bf16[8,8,48,1536]{3,2,0,1:T(8,128)(2,1)}, u32[]{:S(2)}, u32[]{:S(2)}) async-start(bf16[8,8,48,1536]{3,2,0,1:T(8,128)(2,1)} %copy.47), calls=%async_computation.1 | async-start | bytes 18874368 | tf_op jit(solution)/shard_map/all_to_all | solution.py:39
  250.4 110.9 %all-to-all-start.3 = ((bf16[8,8,48,1536]{3,2,0,1:T(8,128)(2,1)}), bf16[8,8,48,1536]{3,2,0,1:T(8,128)(2,1)}, u32[]{:S(2)}, u32[]{:S(2)}) async-start(bf16[8,8,48,1536]{3,2,0,1:T(8,128)(2,1)} %copy.56), calls=%async_computation.5 | async-start | bytes 18874368 | tf_op jit(solution)/shard_map/all_to_all | solution.py:45
  256.4 268.0 %reduce-scatter.3.cloned.1.call-start = ((), (), s32[]{:S(2)}) async-start(), calls=%async_computation.7 | async-start | bytes 7864320 | tf_op jit(solution)/shard_map/reduce_scatter | solution.py:26
  323.6 44.6 %copy-start.7 = (s32[256,6]{0,1:T(8,128)S(1)}, s32[256,6]{0,1:T(8,128)}, u32[]{:S(2)}) copy-start(s32[256,6]{0,1:T(8,128)} %param.23) | copy-start | bytes 18436
  323.6 44.6 %copy-start.9 = (f32[256,6]{0,1:T(8,128)S(1)}, f32[256,6]{0,1:T(8,128)}, u32[]{:S(2)}) copy-start(f32[256,6]{0,1:T(8,128)} %param.21) | copy-start | bytes 18436
  323.6 45.3 %copy-start.10 = (f32[256,6]{0,1:T(8,128)S(1)}, f32[256,6]{0,1:T(8,128)}, u32[]{:S(2)}) copy-start(f32[256,6]{0,1:T(8,128)} %param.20) | copy-start | bytes 18436
  361.3 111.1 %all-to-all-start.1 = ((bf16[8,8,48,1536]{3,2,0,1:T(8,128)(2,1)}), bf16[8,8,48,1536]{3,2,0,1:T(8,128)(2,1)}, u32[]{:S(2)}, u32[]{:S(2)}) async-start(bf16[8,8,48,1536]{3,2,0,1:T(8,128)(2,1)} %copy.49), calls=%async_computation.2 | async-start | bytes 18874368 | tf_op jit(solution)/shard_map/all_to_all | solution.py:45
  504.2 9.3 %copy-start.2 = (bf16[256,6,1536]{2,1,0:T(8,128)(2,1)S(1)}, bf16[256,6,1536]{2,1,0:T(8,128)(2,1)}, u32[]{:S(2)}) copy-start(bf16[256,6,1536]{2,1,0:T(8,128)(2,1)} %reshape.68) | copy-start | bytes 14155780
  504.2 17.0 %copy-start.3 = (bf16[256,1536]{1,0:T(8,128)(2,1)S(1)}, bf16[256,1536]{1,0:T(8,128)(2,1)}, u32[]{:S(2)}) copy-start(bf16[256,1536]{1,0:T(8,128)(2,1)} %param.17) | copy-start | bytes 2359300
  513.6 10.8 %copy-start.5 = (bf16[256,1536]{1,0:T(8,128)(2,1)S(1)}, bf16[256,1536]{1,0:T(8,128)(2,1)}, u32[]{:S(2)}) copy-start(bf16[256,1536]{1,0:T(8,128)(2,1)} %param.16) | copy-start | bytes 2359300
  513.6 14.0 %copy-start.1 = (bf16[256,1536]{1,0:T(8,128)(2,1)S(1)}, bf16[256,1536]{1,0:T(8,128)(2,1)}, u32[]{:S(2)}) copy-start(bf16[256,1536]{1,0:T(8,128)(2,1)} %param.26) | copy-start | bytes 2359300
Sparse Core Ops, SparseCore 0:
  9.6 40.3 all-gather.4
  51.6 36.9 all-gather.2
  90.9 61.7 reduce-scatter.4
  267.5 63.4 reduce-scatter.2
where the time goes:
time: 541 us; the launch traced here: 535 us
  waiting for transfers between devices  235 us (43%)
  local copies, waits for them, and re-layouts  114 us (21%)
  matrix products  112 us (21%)
  other arithmetic  32.5 us (6%)
  starting transfers between devices  26.7 us (5%)
  between operations  14.6 us (3%)
    all_to_all x2, waiting for transfers between devices, routed_path(): lax.all_to_all(send_rows.reshape(local_experts, ep_size, cap_rows, model_...  110 us
    all_to_all x2, waiting for transfers between devices, routed_path(): lax.all_to_all(expert_out.reshape(local_experts, ep_size, cap_rows, model...  109 us
    dot_general x2, matrix products, routed_path(): jnp.einsum('erf,efd->erd', hidden, routed_w2, preferred_element_type=jnp....  53.5 us
    gather x4, local copies, waits for them, and re-layouts, routed_path(): jnp.take(back_rows.reshape(num_rows, model_dim), jnp.maximum(row_ids, 0),...  47.2 us
    dot_general x2, matrix products, routed_path(): jnp.einsum('erd,edf->erf', recv_rows, routed_w1, preferred_element_type=j...  25.9 us
    reduce_sum x2, other arithmetic, routed_path(): return jnp.sum(picked.astype(jnp.float32) * weights[:, :, None], axis=1)  17 us
    all_to_all x2, local copies, waits for them, and re-layouts, routed_path(): lax.all_to_all(send_rows.reshape(local_experts, ep_size, cap_rows, model_...  16.5 us
    all_to_all x2, local copies, waits for them, and re-layouts, routed_path(): lax.all_to_all(expert_out.reshape(local_experts, ep_size, cap_rows, model...  16.5 us
  transfers between devices with their start and end apart: 8, of which 5 were waited for; matrix products, arithmetic and copies ran while one was open for 48% of the time, Pallas kernels for 0%

commit v1 on v0

v1 whole, which is shorter than its diff:
```python
import functools

import jax
import jax.numpy as jnp
from jax import lax
from jax.experimental import pallas as pl
from jax.experimental.pallas import tpu as pltpu
from jax.sharding import PartitionSpec as P

MESH = pl.DeviceIdType.MESH
CORES = 2
TOP_ROWS = 8
FAR, NEXT, PREV, OWN = 0, 1, 2, 3
SERVICE_AT = 4


def capacity_rows(tok_local, top_k, num_experts):
    return max(4, (2 * tok_local * top_k) // num_experts)


def split_three(value):
    hi = value.astype(jnp.bfloat16)
    rest = value - hi.astype(jnp.float32)
    mid = rest.astype(jnp.bfloat16)
    low = (rest - mid.astype(jnp.float32)).astype(jnp.bfloat16)
    return hi, mid, low


def layer_kernel(cfg, meta_in, ta, tb, s1, s3, s2, w1, w3, w2, out_a, out_b, g1, g3, g2,
                 tok, meta, xr, rp, w1b, w3b, w2b, part, rs1, rfull,
                 loc_sem, w_sem, tx_send, tx_recv, tp_send, tp_recv, mt_send, mt_recv,
                 y_send, y_recv, r_send, r_recv, c_send, c_recv, out_sem, free_sem):
    top_k, ep_size, tp_size, cap = cfg
    n_loc = w1.shape[0]
    ff = w1.shape[2]
    sh = s1.shape[1]
    rows, width = ta.shape
    half = rows // 2
    exp_rows = n_loc * cap
    nx = ep_size // CORES
    ep = lax.axis_index('ep')
    ty = lax.axis_index('tp')
    core = ep % CORES
    chip = ep // CORES
    partner = chip * CORES + (1 - core)
    x_next = ((chip + 1) % nx) * CORES + core
    x_prev = ((chip + nx - 1) % nx) * CORES + core
    y_next = (ty + 1) % tp_size
    y_prev = (ty + tp_size - 1) % tp_size
    to_xn, to_xp, to_pr = {'ep': x_next}, {'ep': x_prev}, {'ep': partner}
    to_yn, to_yp = {'tp': y_next}, {'tp': y_prev}
    lo, hi = pl.ds(0, half), pl.ds(half, half)

    def remote(src, dst, ssem, rsem, dev):
        return pltpu.make_async_remote_copy(src_ref=src, dst_ref=dst, send_sem=ssem, recv_sem=rsem,
                                            device_id=dev, device_id_type=MESH)

    def own_sends(m):
        return [remote(tok.at[m, OWN, lo], tok.at[m, PREV, lo], tx_send.at[m, 0], tx_recv.at[m, 0], to_xn),
                remote(tok.at[m, OWN, hi], tok.at[m, NEXT, hi], tx_send.at[m, 3], tx_recv.at[m, 3], to_xp),
                remote(tok.at[m, OWN, hi], tok.at[m, PREV, hi], tx_send.at[m, 1], tx_recv.at[m, 1], to_xn),
                remote(tok.at[m, OWN, lo], tok.at[m, NEXT, lo], tx_send.at[m, 2], tx_recv.at[m, 2], to_xp)]

    def forwards(m):
        return [remote(tok.at[m, PREV, lo], tok.at[m, FAR, lo], tx_send.at[m, 4], tx_recv.at[m, 4], to_xn),
                remote(tok.at[m, NEXT, hi], tok.at[m, FAR, hi], tx_send.at[m, 5], tx_recv.at[m, 5], to_xp)]

    def to_partner(m, k):
        return remote(tok.at[m, k], tok.at[m, k + 4], tp_send.at[m, k], tp_recv.at[m, k], to_pr)

    meta_next = remote(meta.at[OWN], meta.at[PREV], mt_send.at[0], mt_recv.at[0], to_xn)
    meta_prev = remote(meta.at[OWN], meta.at[NEXT], mt_send.at[1], mt_recv.at[1], to_xp)
    meta_far = remote(meta.at[PREV], meta.at[FAR], mt_send.at[2], mt_recv.at[2], to_xn)
    meta_pair = [remote(meta.at[k], meta.at[k + 4], mt_send.at[3 + k], mt_recv.at[3 + k], to_pr) for k in range(4)]
    y_own = []
    for i, (src, dst) in enumerate(((s1, g1), (s2, g2), (s3, g3))):
        y_own.append(remote(src, dst.at[PREV], y_send.at[i], y_recv.at[i], to_yn))
        y_own.append(remote(src, dst.at[NEXT], y_send.at[3 + i], y_recv.at[3 + i], to_yp))
    y_far = [remote(g1.at[PREV], g1.at[FAR], y_send.at[6], y_recv.at[6], to_yn),
             remote(g2.at[PREV], g2.at[FAR], y_send.at[7], y_recv.at[7], to_yn),
             remote(g3.at[NEXT], g3.at[FAR], y_send.at[8], y_recv.at[8], to_yp)]

    def weights(e, slot):
        return [pltpu.make_async_copy(w1.at[e], w1b.at[slot], w_sem.at[slot, 0]),
                pltpu.make_async_copy(w3.at[e], w3b.at[slot], w_sem.at[slot, 1]),
                pltpu.make_async_copy(w2.at[e], w2b.at[slot], w_sem.at[slot, 2])]

    def push_rows(m, e):
        return remote(xr.at[e, pl.ds(4, 4)], rp.at[e], r_send.at[m, e], r_recv.at[m, e], to_pr)

    def first_far(m):
        return [remote(part.at[m, FAR, hi], rs1.at[m, 0], c_send.at[m, 0], c_recv.at[m, 0], to_xn),
                remote(part.at[m, FAR, lo], rs1.at[m, 1], c_send.at[m, 1], c_recv.at[m, 1], to_xp)]

    def near_own(m):
        return [remote(part.at[m, NEXT, lo], rfull.at[m, 0, lo], c_send.at[m, 2], c_recv.at[m, 2], to_xn),
                remote(part.at[m, PREV, hi], rfull.at[m, 1, hi], c_send.at[m, 3], c_recv.at[m, 3], to_xp)]

    def near_sum(m):
        return [remote(part.at[m, NEXT, hi], rfull.at[m, 0, hi], c_send.at[m, 4], c_recv.at[m, 4], to_xn),
                remote(part.at[m, PREV, lo], rfull.at[m, 1, lo], c_send.at[m, 5], c_recv.at[m, 5], to_xp)]

    local = [pltpu.make_async_copy(meta_in, meta.at[OWN], loc_sem.at[0]),
             pltpu.make_async_copy(ta, tok.at[0, OWN], loc_sem.at[1]),
             pltpu.make_async_copy(tb, tok.at[1, OWN], loc_sem.at[2])]
    for cp in local + weights(0, 0):
        cp.start()
    barrier = pltpu.get_barrier_semaphore()
    for dev in (to_xn, to_xp, to_pr, to_yn, to_yp):
        pl.semaphore_signal(barrier, inc=1, device_id=dev, device_id_type=MESH)
    for cp in local:
        cp.wait()
    pl.semaphore_wait(barrier, 5)

    for cp in [meta_next, meta_prev, meta_pair[OWN]] + own_sends(0) + [to_partner(0, OWN)]:
        cp.start()
    for cp in y_own:
        cp.start()
    sent = own_sends(0)
    sent[0].wait_recv()
    sent[1].wait_recv()
    for cp in forwards(0):
        cp.start()
    meta_next.wait_recv()
    meta_prev.wait_recv()
    meta_far.start()
    for cp in own_sends(1) + [to_partner(1, OWN), meta_pair[NEXT], meta_pair[PREV]]:
        cp.start()
    sent[2].wait_recv()
    sent[3].wait_recv()
    to_partner(0, NEXT).start()
    to_partner(0, PREV).start()
    meta_far.wait_recv()
    meta_pair[FAR].start()
    for cp in forwards(0):
        cp.wait_recv()
    to_partner(0, FAR).start()
    for k in range(4):
        meta_pair[k].wait_recv()
        to_partner(0, k).wait_recv()

    row_id = lax.broadcasted_iota(jnp.int32, (exp_rows, rows), 0).astype(jnp.float32)

    def placed(ids, base, values):
        shifted = row_id + (base * exp_rows).astype(jnp.float32)
        total = jnp.zeros((exp_rows, rows), jnp.float32)
        for j in range(top_k):
            total = jnp.where(shifted == ids[j:j + 1, :], 1.0 if values is None else values[j:j + 1, :], total)
        return total

    def gather(m):
        def one(k, carry):
            ids = meta[k, m, pl.ds(0, TOP_ROWS), :]
            place = placed(ids, ep, None).astype(jnp.bfloat16)
            got = jnp.dot(place, tok[m, k], preferred_element_type=jnp.float32).astype(jnp.bfloat16)
            xr[:, k] = got.reshape(n_loc, cap, width)
            return carry
        lax.fori_loop(0, 8, one, 0)

    def swiglu(x_rows, slot):
        proj_in = jnp.dot(x_rows, w1b[slot], preferred_element_type=jnp.float32)
        proj_gate = jnp.dot(x_rows, w3b[slot], preferred_element_type=jnp.float32)
        hidden = (jax.nn.silu(proj_in) * proj_gate).astype(jnp.bfloat16)
        return jnp.dot(hidden, w2b[slot], preferred_element_type=jnp.float32)

    def experts(m):
        def one(e, carry):
            slot = e % 2

            def prefetch():
                for cp in weights((e + 1) % n_loc, 1 - slot):
                    cp.start()
            if m == 0:
                prefetch()
            else:
                pl.when(e < n_loc - 1)(prefetch)

            @pl.when(e > 0)
            def _():
                push_rows(m, e - 1).start()
            for cp in weights(e, slot):
                cp.wait()
            res = swiglu(xr[e].reshape(8 * cap, width), slot).astype(jnp.bfloat16)
            xr[e] = res.reshape(8, cap, width)
            if m == 0:
                @pl.when(e == SERVICE_AT)
                def _():
                    s = own_sends(1)
                    s[0].wait_recv()
                    s[1].wait_recv()
                    for cp in forwards(1):
                        cp.start()
                    s[2].wait_recv()
                    s[3].wait_recv()
                    to_partner(1, NEXT).start()
                    to_partner(1, PREV).start()
            return carry
        lax.fori_loop(0, n_loc, one, 0)
        push_rows(m, n_loc - 1).start()

    def combine(m):
        for e in range(n_loc):
            push_rows(m, e).wait_recv()

        def one(i, carry):
            ids = meta[i, m, pl.ds(0, TOP_ROWS), :]
            vals = meta[i, m, pl.ds(TOP_ROWS, TOP_ROWS), :]
            mine = jnp.concatenate(split_three(placed(ids, ep, vals).T), axis=0)
            other = jnp.concatenate(split_three(placed(ids, partner, vals).T), axis=0)
            for n in range(width // 256):
                cols = pl.ds(n * 256, 256)
                acc = jnp.dot(mine, xr[:, i, :, cols].reshape(exp_rows, 256), preferred_element_type=jnp.float32)
                acc = acc + jnp.dot(other, rp[:, i, :, cols].reshape(exp_rows, 256), preferred_element_type=jnp.float32)
                part[m, i, :, cols] = acc[0:rows] + acc[rows:2 * rows] + acc[2 * rows:3 * rows]

            @pl.when(i == 1)
            def _():
                for cp in first_far(m):
                    cp.start()

            @pl.when(i == 2)
            def _():
                near_own(m)[0].start()

            @pl.when(i == 3)
            def _():
                near_own(m)[1].start()
            return carry
        lax.fori_loop(0, 4, one, 0)

    def pass_on(m):
        first = first_far(m)
        sends = near_sum(m)
        first[0].wait_recv()
        part[m, NEXT, hi] = part[m, NEXT, hi] + rs1[m, 0]
        first[1].wait_recv()
        part[m, PREV, lo] = part[m, PREV, lo] + rs1[m, 1]
        sends[0].start()
        sends[1].start()

    def finish(m, out):
        for cp in own_sends(m) + [to_partner(m, OWN)]:
            cp.wait_send()
        for cp in near_own(m) + near_sum(m):
            cp.wait_recv()
        total = part[m, OWN] + tok[m, OWN].astype(jnp.float32) + rfull[m, 0] + rfull[m, 1]
        tok[m, OWN] = total.astype(jnp.bfloat16)
        cp = pltpu.make_async_copy(tok.at[m, OWN], out, out_sem.at[m])
        cp.start()
        return cp

    gather(0)
    experts(0)
    for cp in forwards(1):
        cp.wait_recv()
    to_partner(1, FAR).start()
    combine(0)
    pl.semaphore_signal(free_sem, inc=1, device_id=to_pr, device_id_type=MESH)
    for cp in y_own:
        cp.wait_recv()
    for cp in y_far:
        cp.start()
    for k in range(4):
        to_partner(1, k).wait_recv()
    for e in range(n_loc):
        push_rows(0, e).wait_send()
    gather(1)
    pl.semaphore_wait(free_sem, 1)
    experts(1)
    pass_on(0)
    for cp in y_far:
        cp.wait_recv()
    shared = []
    for slot, pair in enumerate((((s1, s3, s2), NEXT), (None, FAR))):
        srcs = [pair[0] or (g1.at[PREV], g3.at[PREV], g2.at[PREV]), (g1.at[pair[1]], g3.at[pair[1]], g2.at[pair[1]])]
        for p, (a1, a3, a2) in enumerate(srcs):
            part_of = pl.ds(p * sh, sh)
            shared.append(pltpu.make_async_copy(a1, w1b.at[slot, :, part_of], w_sem.at[slot, 3 + p]))
            shared.append(pltpu.make_async_copy(a3, w3b.at[slot, :, part_of], w_sem.at[slot, 5 + p]))
            shared.append(pltpu.make_async_copy(a2, w2b.at[slot, part_of, :], w_sem.at[slot, 7 + p]))
    for cp in shared:
        cp.start()
    combine(1)
    for cp in shared:
        cp.wait()

    def shared_one(i, carry):
        m = i // 2
        part[m, OWN] = part[m, OWN] + swiglu(tok[m, OWN], i % 2)
        return carry
    lax.fori_loop(0, 4, shared_one, 0)

    done_a = finish(0, out_a)
    pass_on(1)
    done_b = finish(1, out_b)
    for m in range(2):
        for k in range(3):
            to_partner(m, k).wait_send()
        for cp in forwards(m) + first_far(m) + near_own(m) + near_sum(m):
            cp.wait_send()
    for e in range(n_loc):
        push_rows(1, e).wait_send()
    for cp in [meta_next, meta_prev, meta_far] + meta_pair + y_own + y_far:
        cp.wait_send()
    done_a.wait()
    done_b.wait()


def solution(mesh):
    ep_size = mesh.shape['ep']
    tp_size = mesh.shape['tp']
    tok_spec = P(('data', 'ep', 'tp'), None)
    in_specs = (tok_spec,) * 8 + (P(None, 'tp'), P(None, 'tp'), P('tp', None), P('ep', None, None), P('ep', None, None), P('ep', None, None))

    def routing_rows(expert_ids, gate_vals, slot_ids, cap):
        keep = slot_ids >= 0
        ids = jnp.where(keep, expert_ids * cap + slot_ids, -1).astype(jnp.float32).T
        vals = jnp.where(keep, gate_vals, 0.0).T
        pad = ((0, TOP_ROWS - ids.shape[0]), (0, 0))
        return jnp.concatenate([jnp.pad(ids, pad, constant_values=-1.0), jnp.pad(vals, pad)], axis=0)

    def layer_local(tokens_a, tokens_b, experts_a, experts_b, gates_a, gates_b, slots_a, slots_b, shared_w1, shared_w3, shared_w2, routed_w1, routed_w3, routed_w2):
        rows, width = tokens_a.shape
        top_k = experts_a.shape[1]
        n_loc, _, ff = routed_w1.shape
        sh = shared_w1.shape[1]
        cap = capacity_rows(rows, top_k, n_loc * ep_size)
        half = rows // 2
        meta = jnp.stack([routing_rows(experts_a, gates_a, slots_a, cap), routing_rows(experts_b, gates_b, slots_b, cap)])
        bf, f32 = jnp.bfloat16, jnp.float32
        dma = pltpu.SemaphoreType.DMA
        any_spec = pl.BlockSpec(memory_space=pl.ANY)
        outs = pl.pallas_call(
            functools.partial(layer_kernel, (top_k, ep_size, tp_size, cap)),
            out_shape=(jax.ShapeDtypeStruct((rows, width), bf), jax.ShapeDtypeStruct((rows, width), bf),
                       jax.ShapeDtypeStruct((3, width, sh), bf), jax.ShapeDtypeStruct((3, width, sh), bf),
                       jax.ShapeDtypeStruct((3, sh, width), bf)),
            in_specs=[any_spec] * 9,
            out_specs=[any_spec] * 5,
            scratch_shapes=[
                pltpu.VMEM((2, 8, rows, width), bf),
                pltpu.VMEM((8, 2, 2 * TOP_ROWS, rows), f32),
                pltpu.VMEM((n_loc, 8, cap, width), bf),
                pltpu.VMEM((n_loc, 4, cap, width), bf),
                pltpu.VMEM((2, width, ff), bf),
                pltpu.VMEM((2, width, ff), bf),
                pltpu.VMEM((2, ff, width), bf),
                pltpu.VMEM((2, 4, rows, width), f32),
                pltpu.VMEM((2, 2, half, width), f32),
                pltpu.VMEM((2, 2, rows, width), f32),
                dma((3,)), dma((2, 9)), dma((2, 6)), dma((2, 6)), dma((2, 4)), dma((2, 4)), dma((7,)), dma((7,)),
                dma((9,)), dma((9,)), dma((2, n_loc)), dma((2, n_loc)), dma((2, 6)), dma((2, 6)), dma((2,)),
                pltpu.SemaphoreType.REGULAR,
            ],
            compiler_params=pltpu.CompilerParams(collective_id=0, has_side_effects=True, vmem_limit_bytes=67043328),
        )(meta, tokens_a, tokens_b, shared_w1, shared_w3, shared_w2, routed_w1, routed_w3, routed_w2)
        return outs[0], outs[1]

    return jax.shard_map(layer_local, mesh=mesh, in_specs=in_specs, out_specs=(tok_spec, tok_spec), check_vma=False)
```

time: 541 us -> 183 us (0.34); the launches traced: 535 us -> 182 us
  waiting for transfers between devices: 235 us -> 0 us
  Pallas kernels: 0 us -> 174 us
  matrix products: 112 us -> 0 us
  local copies, waits for them, and re-layouts: 114 us -> 4.13 us
  other arithmetic: 32.5 us -> 3.5 us
  starting transfers between devices: 26.7 us -> 0 us
  between operations: 14.6 us -> 0.64 us
    all_to_all x4 -> x0, waiting for transfers between devices: 219 us -> none  [the longest x2 110 us: routed_path(): lax.all_to_all(send_rows.reshape(local_experts, ep_size, cap_rows, model_...]
    pallas_call x0 -> x1, Pallas kernels: none -> 174 us  [layer_local(): pl.pallas_call(functools.partial(layer_kernel, (top_k, ep_size, tp_size,...]
    dot_general x10 -> x0, matrix products: 112 us -> none  [the longest x2 53.5 us: routed_path(): jnp.einsum('erf,efd->erd', hidden, routed_w2, preferred_element_type=jnp....]
    gather x4 -> x0, local copies, waits for them, and re-layouts: 47.2 us -> none  [routed_path(): jnp.take(back_rows.reshape(num_rows, model_dim), jnp.maximum(row_ids, 0),...]
    all_to_all x4 -> x0, local copies, waits for them, and re-layouts: 33 us -> none  [the longest x2 16.5 us: routed_path(): lax.all_to_all(send_rows.reshape(local_experts, ep_size, cap_rows, model_...]
    reshape x4 -> x0, local copies, waits for them, and re-layouts: 32.8 us -> none  [the longest x2 16.4 us: routed_path(): expert_out.reshape(local_experts, ep_size, cap_rows, model_dim)]
    all_to_all x4 -> x0, starting transfers between devices: 25.9 us -> none  [the longest x2 13.5 us: routed_path(): lax.all_to_all(send_rows.reshape(local_experts, ep_size, cap_rows, model_...]
    reduce_sum x2 -> x0, other arithmetic: 17 us -> none  [routed_path(): return jnp.sum(picked.astype(jnp.float32) * weights[:, :, None], axis=1)]
  transfers between devices with their start and end apart: 8 -> 0, of which waited for: 5 -> 0; matrix products, arithmetic and copies ran while one was open for 48% -> 0% of each run, Pallas kernels for 0% -> 0%
where the time goes in v1:
time: 183 us; the launch traced here: 182 us
  Pallas kernels  174 us (95%)
  local copies, waits for them, and re-layouts  4.13 us (2%)
  other arithmetic  3.5 us (2%)
    pallas_call x1, Pallas kernels, layer_local(): pl.pallas_call(functools.partial(layer_kernel, (top_k, ep_size, tp_size,...  174 us
    unnamed x2, local copies, waits for them, and re-layouts  4.13 us

profile of v1, /device:TPU:97, one launch (start us, length us, event | category | flops | bytes accessed | tf_op | source)
XLA Modules:
  0.0 182.5 jit_solution(11793296044009298545)
XLA Ops:
  0.6 0.7 convert_bitcast_fusion.1
  1.4 0.7 convert_bitcast_fusion
  2.1 0.7 select_bitcast_fusion.1
  2.8 0.7 select_bitcast_fusion
  3.5 0.6 pad_maximum_fusion.meta_in
  4.1 174.2 %shard_map.149 = (bf16[256,1536]{1,0:T(8,128)(2,1)}, bf16[256,1536]{1,0:T(8,128)(2,1)}, bf16[3,1536,256]{2,1,0:T(8,128)(2,1)}, bf16[3,1536,256]{2,1,0:T(8,128)(2,1)}, bf16[3,256,1536]{2,1,0:T(8,128)(2,1)}) custom-call(f32[2,16,256]{2,1,0:T(8,128)} %pad_maximum_fusion.meta_in, bf16[256,1536]{1,0:T(8,128)(2,1)} %ta.1, bf16[256,1536]{1,0:T(8,128)(2,1)} %tb.1, ...), custom_call_target="tpu_custom_call" | custom-call | tf_op jit(solution)/shard_map/pallas_call | solution.py:333
  178.3 2.1 %copy.18 = bf16[256,1536]{1,0:T(8,128)(2,1)} copy(bf16[256,1536]{1,0:T(8,128)(2,1)} %get-tuple-element.10) | data formatting | bytes 1572864
  180.4 2.1 %copy.19 = bf16[256,1536]{1,0:T(8,128)(2,1)} copy(bf16[256,1536]{1,0:T(8,128)(2,1)} %get-tuple-element.11) | data formatting | bytes 1572864
  (1 shorter events, 0.0 us)

commit v2 on v1

--- a/solution.py
+++ b/solution.py
@@ -9,9 +9,7 @@
 
 MESH = pl.DeviceIdType.MESH
 CORES = 2
-TOP_ROWS = 8
-FAR, NEXT, PREV, OWN = 0, 1, 2, 3
-SERVICE_AT = 4
+OWN, NEXT, PREV, FAR = 0, 1, 2, 3
 
 
 def capacity_rows(tok_local, top_k, num_experts):
@@ -26,8 +24,8 @@
     return hi, mid, low
 
 
-def layer_kernel(cfg, meta_in, ta, tb, s1, s3, s2, w1, w3, w2, out_a, out_b, g1, g3, g2,
-                 tok, meta, xr, rp, w1b, w3b, w2b, part, rs1, rfull,
+def layer_kernel(cfg, ea, eb, ga, gb, sa, sb, ta, tb, s1, s3, s2, w1, w3, w2, out_a, out_b, g1, g3, g2,
+                 tok, mids, mval, xr, rp, w1b, w3b, w2b, part, rs1, rfull,
                  loc_sem, w_sem, tx_send, tx_recv, tp_send, tp_recv, mt_send, mt_recv,
                  y_send, y_recv, r_send, r_recv, c_send, c_recv, out_sem, free_sem):
     top_k, ep_size, tp_size, cap = cfg
@@ -68,17 +66,21 @@
     def to_partner(m, k):
         return remote(tok.at[m, k], tok.at[m, k + 4], tp_send.at[m, k], tp_recv.at[m, k], to_pr)
 
-    meta_next = remote(meta.at[OWN], meta.at[PREV], mt_send.at[0], mt_recv.at[0], to_xn)
-    meta_prev = remote(meta.at[OWN], meta.at[NEXT], mt_send.at[1], mt_recv.at[1], to_xp)
-    meta_far = remote(meta.at[PREV], meta.at[FAR], mt_send.at[2], mt_recv.at[2], to_xn)
-    meta_pair = [remote(meta.at[k], meta.at[k + 4], mt_send.at[3 + k], mt_recv.at[3 + k], to_pr) for k in range(4)]
+    def meta(i, src, dst, dev):
+        return [remote(mids.at[src], mids.at[dst], mt_send.at[0, i], mt_recv.at[0, i], dev),
+                remote(mval.at[src], mval.at[dst], mt_send.at[1, i], mt_recv.at[1, i], dev)]
+
+    meta_next = meta(0, OWN, PREV, to_xn)
+    meta_prev = meta(1, OWN, NEXT, to_xp)
+    meta_far = meta(2, PREV, FAR, to_xn)
+    meta_pair = [meta(3 + k, k, k + 4, to_pr) for k in range(4)]
     y_own = []
     for i, (src, dst) in enumerate(((s1, g1), (s2, g2), (s3, g3))):
-        y_own.append(remote(src, dst.at[PREV], y_send.at[i], y_recv.at[i], to_yn))
-        y_own.append(remote(src, dst.at[NEXT], y_send.at[3 + i], y_recv.at[3 + i], to_yp))
-    y_far = [remote(g1.at[PREV], g1.at[FAR], y_send.at[6], y_recv.at[6], to_yn),
-             remote(g2.at[PREV], g2.at[FAR], y_send.at[7], y_recv.at[7], to_yn),
-             remote(g3.at[NEXT], g3.at[FAR], y_send.at[8], y_recv.at[8], to_yp)]
+        y_own.append(remote(src, dst.at[PREV - 1], y_send.at[i], y_recv.at[i], to_yn))
+        y_own.append(remote(src, dst.at[NEXT - 1], y_send.at[3 + i], y_recv.at[3 + i], to_yp))
+    y_far = [remote(g1.at[PREV - 1], g1.at[FAR - 1], y_send.at[6], y_recv.at[6], to_yn),
+             remote(g2.at[PREV - 1], g2.at[FAR - 1], y_send.at[7], y_recv.at[7], to_yn),
+             remote(g3.at[NEXT - 1], g3.at[FAR - 1], y_send.at[8], y_recv.at[8], to_yp)]
 
     def weights(e, slot):
         return [pltpu.make_async_copy(w1.at[e], w1b.at[slot], w_sem.at[slot, 0]),
@@ -100,58 +102,77 @@
         return [remote(part.at[m, NEXT, hi], rfull.at[m, 0, hi], c_send.at[m, 4], c_recv.at[m, 4], to_xn),
                 remote(part.at[m, PREV, lo], rfull.at[m, 1, lo], c_send.at[m, 5], c_recv.at[m, 5], to_xp)]
 
-    local = [pltpu.make_async_copy(meta_in, meta.at[OWN], loc_sem.at[0]),
-             pltpu.make_async_copy(ta, tok.at[0, OWN], loc_sem.at[1]),
-             pltpu.make_async_copy(tb, tok.at[1, OWN], loc_sem.at[2])]
-    for cp in local + weights(0, 0):
-        cp.start()
+    local = [pltpu.make_async_copy(src, dst, loc_sem.at[i]) for i, (src, dst) in enumerate((
+        (ta, tok.at[0, OWN]), (ea, mids.at[OWN, 0, 0]), (sa, mids.at[OWN, 0, 1]), (ga, mval.at[OWN, 0]),
+        (eb, mids.at[OWN, 1, 0]), (sb, mids.at[OWN, 1, 1]), (gb, mval.at[OWN, 1]), (tb, tok.at[1, OWN])))]
     barrier = pltpu.get_barrier_semaphore()
     for dev in (to_xn, to_xp, to_pr, to_yn, to_yp):
         pl.semaphore_signal(barrier, inc=1, device_id=dev, device_id_type=MESH)
     for cp in local:
+        cp.start()
+    for cp in local[:-1]:
         cp.wait()
     pl.semaphore_wait(barrier, 5)
-
-    for cp in [meta_next, meta_prev, meta_pair[OWN]] + own_sends(0) + [to_partner(0, OWN)]:
-        cp.start()
-    for cp in y_own:
-        cp.start()
-    sent = own_sends(0)
-    sent[0].wait_recv()
-    sent[1].wait_recv()
-    for cp in forwards(0):
-        cp.start()
-    meta_next.wait_recv()
-    meta_prev.wait_recv()
-    meta_far.start()
-    for cp in own_sends(1) + [to_partner(1, OWN), meta_pair[NEXT], meta_pair[PREV]]:
-        cp.start()
-    sent[2].wait_recv()
-    sent[3].wait_recv()
-    to_partner(0, NEXT).start()
-    to_partner(0, PREV).start()
-    meta_far.wait_recv()
-    meta_pair[FAR].start()
-    for cp in forwards(0):
-        cp.wait_recv()
-    to_partner(0, FAR).start()
-    for k in range(4):
-        meta_pair[k].wait_recv()
-        to_partner(0, k).wait_recv()
-
-    row_id = lax.broadcasted_iota(jnp.int32, (exp_rows, rows), 0).astype(jnp.float32)
+    first = own_sends(0)
+    for cp in meta_next + meta_prev + first + meta_pair[OWN] + [to_partner(0, OWN)]:
+        cp.start()
+    for cp in y_own + weights(0, 0):
+        cp.start()
+    local[-1].wait()
+
+    row_id = lax.broadcasted_iota(jnp.int32, (exp_rows, rows), 0)
 
     def placed(ids, base, values):
-        shifted = row_id + (base * exp_rows).astype(jnp.float32)
+        shifted = row_id + base * exp_rows
         total = jnp.zeros((exp_rows, rows), jnp.float32)
         for j in range(top_k):
             total = jnp.where(shifted == ids[j:j + 1, :], 1.0 if values is None else values[j:j + 1, :], total)
         return total
 
+    def row_ids(k, m):
+        slot = mids[k, m, 1]
+        return jnp.where(slot >= 0, mids[k, m, 0] * cap + slot, -1)
+
+    def arrivals(step):
+        if step == 1:
+            for cp in meta_pair[OWN] + [to_partner(0, OWN)]:
+                cp.wait_recv()
+        elif step == 2:
+            first[0].wait_recv()
+            first[1].wait_recv()
+            for cp in forwards(0):
+                cp.start()
+            for cp in meta_next + meta_prev:
+                cp.wait_recv()
+            for cp in meta_far + own_sends(1) + meta_pair[NEXT] + meta_pair[PREV] + [to_partner(1, OWN)]:
+                cp.start()
+            first[2].wait_recv()
+            first[3].wait_recv()
+            to_partner(0, NEXT).start()
+            to_partner(0, PREV).start()
+        elif step in (3, 5):
+            k = NEXT if step == 3 else PREV
+            for cp in meta_pair[k] + [to_partner(0, k)]:
+                cp.wait_recv()
+        elif step == 6:
+            for cp in meta_far:
+                cp.wait_recv()
+            for cp in meta_pair[FAR]:
+                cp.start()
+            for cp in forwards(0):
+                cp.wait_recv()
+            to_partner(0, FAR).start()
+        elif step == 7:
+            for cp in meta_pair[FAR] + [to_partner(0, FAR)]:
+                cp.wait_recv()
+
     def gather(m):
-        def one(k, carry):
-            ids = meta[k, m, pl.ds(0, TOP_ROWS), :]
-            place = placed(ids, ep, None).astype(jnp.bfloat16)
+        def one(step, carry):
+            if m == 0:
+                for at in range(1, 8):
+                    pl.when(step == at)(functools.partial(arrivals, at))
+            k = (step % 2) * 4 + step // 2
+            place = placed(row_ids(k, m), ep, None).astype(jnp.bfloat16)
             got = jnp.dot(place, tok[m, k], preferred_element_type=jnp.float32).astype(jnp.bfloat16)
             xr[:, k] = got.reshape(n_loc, cap, width)
             return carry
@@ -162,6 +183,19 @@
         proj_gate = jnp.dot(x_rows, w3b[slot], preferred_element_type=jnp.float32)
         hidden = (jax.nn.silu(proj_in) * proj_gate).astype(jnp.bfloat16)
         return jnp.dot(hidden, w2b[slot], preferred_element_type=jnp.float32)
+
+    def second_arrivals(step):
+        sends = own_sends(1)
+        if step == 0:
+            sends[0].wait_recv()
+            sends[1].wait_recv()
+            for cp in forwards(1):
+                cp.start()
+        else:
+            sends[2].wait_recv()
+            sends[3].wait_recv()
+            to_partner(1, NEXT).start()
+            to_partner(1, PREV).start()
 
     def experts(m):
         def one(e, carry):
@@ -183,17 +217,8 @@
             res = swiglu(xr[e].reshape(8 * cap, width), slot).astype(jnp.bfloat16)
             xr[e] = res.reshape(8, cap, width)
             if m == 0:
-                @pl.when(e == SERVICE_AT)
-                def _():
-                    s = own_sends(1)
-                    s[0].wait_recv()
-                    s[1].wait_recv()
-                    for cp in forwards(1):
-                        cp.start()
-                    s[2].wait_recv()
-                    s[3].wait_recv()
-                    to_partner(1, NEXT).start()
-                    to_partner(1, PREV).start()
+                pl.when(e == n_loc // 2 - 1)(functools.partial(second_arrivals, 0))
+                pl.when(e == n_loc - 2)(functools.partial(second_arrivals, 1))
             return carry
         lax.fori_loop(0, n_loc, one, 0)
         push_rows(m, n_loc - 1).start()
@@ -202,9 +227,10 @@
         for e in range(n_loc):
             push_rows(m, e).wait_recv()
 
-        def one(i, carry):
-            ids = meta[i, m, pl.ds(0, TOP_ROWS), :]
-            vals = meta[i, m, pl.ds(TOP_ROWS, TOP_ROWS), :]
+        def one(step, carry):
+            i = 3 - step
+            ids = row_ids(i, m)
+            vals = jnp.where(mids[i, m, 1] >= 0, mval[i, m], 0.0)
             mine = jnp.concatenate(split_three(placed(ids, ep, vals).T), axis=0)
             other = jnp.concatenate(split_three(placed(ids, partner, vals).T), axis=0)
             for n in range(width // 256):
@@ -213,27 +239,27 @@
                 acc = acc + jnp.dot(other, rp[:, i, :, cols].reshape(exp_rows, 256), preferred_element_type=jnp.float32)
                 part[m, i, :, cols] = acc[0:rows] + acc[rows:2 * rows] + acc[2 * rows:3 * rows]
 
-            @pl.when(i == 1)
+            @pl.when(step == 0)
             def _():
                 for cp in first_far(m):
                     cp.start()
 
-            @pl.when(i == 2)
+            @pl.when(step == 1)
+            def _():
+                near_own(m)[1].start()
+
+            @pl.when(step == 2)
             def _():
                 near_own(m)[0].start()
-
-            @pl.when(i == 3)
-            def _():
-                near_own(m)[1].start()
             return carry
         lax.fori_loop(0, 4, one, 0)
 
     def pass_on(m):
-        first = first_far(m)
+        incoming = first_far(m)
         sends = near_sum(m)
-        first[0].wait_recv()
+        incoming[0].wait_recv()
         part[m, NEXT, hi] = part[m, NEXT, hi] + rs1[m, 0]
-        first[1].wait_recv()
+        incoming[1].wait_recv()
         part[m, PREV, lo] = part[m, PREV, lo] + rs1[m, 1]
         sends[0].start()
         sends[1].start()
@@ -251,10 +277,10 @@
 
     gather(0)
     experts(0)
+    combine(0)
     for cp in forwards(1):
         cp.wait_recv()
     to_partner(1, FAR).start()
-    combine(0)
     pl.semaphore_signal(free_sem, inc=1, device_id=to_pr, device_id_type=MESH)
     for cp in y_own:
         cp.wait_recv()
@@ -272,7 +298,7 @@
         cp.wait_recv()
     shared = []
     for slot, pair in enumerate((((s1, s3, s2), NEXT), (None, FAR))):
-        srcs = [pair[0] or (g1.at[PREV], g3.at[PREV], g2.at[PREV]), (g1.at[pair[1]], g3.at[pair[1]], g2.at[pair[1]])]
+        srcs = [pair[0] or (g1.at[PREV - 1], g3.at[PREV - 1], g2.at[PREV - 1]), (g1.at[pair[1] - 1], g3.at[pair[1] - 1], g2.at[pair[1] - 1])]
         for p, (a1, a3, a2) in enumerate(srcs):
             part_of = pl.ds(p * sh, sh)
             shared.append(pltpu.make_async_copy(a1, w1b.at[slot, :, part_of], w_sem.at[slot, 3 + p]))
@@ -294,16 +320,28 @@
     pass_on(1)
     done_b = finish(1, out_b)
     for m in range(2):
-        for k in range(3):
+        for k in (NEXT, PREV, FAR):
             to_partner(m, k).wait_send()
         for cp in forwards(m) + first_far(m) + near_own(m) + near_sum(m):
             cp.wait_send()
     for e in range(n_loc):
         push_rows(1, e).wait_send()
-    for cp in [meta_next, meta_prev, meta_far] + meta_pair + y_own + y_far:
+    for cp in meta_next + meta_prev + meta_far + sum(meta_pair, []) + y_own + y_far:
         cp.wait_send()
     done_a.wait()
     done_b.wait()
+
+
+def place_kernel(a, b, out_a, out_b, buf, in_sem, out_sem):
+    loads = [pltpu.make_async_copy(src, buf.at[i], in_sem.at[i]) for i, src in enumerate((a, b))]
+    stores = [pltpu.make_async_copy(buf.at[i], dst, out_sem.at[i]) for i, dst in enumerate((out_a, out_b))]
+    for cp in loads:
+        cp.start()
+    for load, store in zip(loads, stores):
+        load.wait()
+        store.start()
+    for cp in stores:
+        cp.wait()
 
 
 def solution(mesh):
@@ -311,13 +349,6 @@
     tp_size = mesh.shape['tp']
     tok_spec = P(('data', 'ep', 'tp'), None)
     in_specs = (tok_spec,) * 8 + (P(None, 'tp'), P(None, 'tp'), P('tp', None), P('ep', None, None), P('ep', None, None), P('ep', None, None))
-
-    def routing_rows(expert_ids, gate_vals, slot_ids, cap):
-        keep = slot_ids >= 0
-        ids = jnp.where(keep, expert_ids * cap + slot_ids, -1).astype(jnp.float32).T
-        vals = jnp.where(keep, gate_vals, 0.0).T
-        pad = ((0, TOP_ROWS - ids.shape[0]), (0, 0))
-        return jnp.concatenate([jnp.pad(ids, pad, constant_values=-1.0), jnp.pad(vals, pad)], axis=0)
 
     def layer_local(tokens_a, tokens_b, experts_a, experts_b, gates_a, gates_b, slots_a, slots_b, shared_w1, shared_w3, shared_w2, routed_w1, routed_w3, routed_w2):
         rows, width = tokens_a.shape
@@ -326,7 +357,7 @@
         sh = shared_w1.shape[1]
         cap = capacity_rows(rows, top_k, n_loc * ep_size)
         half = rows // 2
-        meta = jnp.stack([routing_rows(experts_a, gates_a, slots_a, cap), routing_rows(experts_b, gates_b, slots_b, cap)])
+        routing = [a.T for a in (experts_a, experts_b, gates_a, gates_b, slots_a, slots_b)]
         bf, f32 = jnp.bfloat16, jnp.float32
         dma = pltpu.SemaphoreType.DMA
         any_spec = pl.BlockSpec(memory_space=pl.ANY)
@@ -335,11 +366,12 @@
             out_shape=(jax.ShapeDtypeStruct((rows, width), bf), jax.ShapeDtypeStruct((rows, width), bf),
                        jax.ShapeDtypeStruct((3, width, sh), bf), jax.ShapeDtypeStruct((3, width, sh), bf),
                        jax.ShapeDtypeStruct((3, sh, width), bf)),
-            in_specs=[any_spec] * 9,
+            in_specs=[any_spec] * 14,
             out_specs=[any_spec] * 5,
             scratch_shapes=[
                 pltpu.VMEM((2, 8, rows, width), bf),
-                pltpu.VMEM((8, 2, 2 * TOP_ROWS, rows), f32),
+                pltpu.VMEM((8, 2, 2, top_k, rows), jnp.int32),
+                pltpu.VMEM((8, 2, top_k, rows), f32),
                 pltpu.VMEM((n_loc, 8, cap, width), bf),
                 pltpu.VMEM((n_loc, 4, cap, width), bf),
                 pltpu.VMEM((2, width, ff), bf),
@@ -348,12 +380,18 @@
                 pltpu.VMEM((2, 4, rows, width), f32),
                 pltpu.VMEM((2, 2, half, width), f32),
                 pltpu.VMEM((2, 2, rows, width), f32),
-                dma((3,)), dma((2, 9)), dma((2, 6)), dma((2, 6)), dma((2, 4)), dma((2, 4)), dma((7,)), dma((7,)),
+                dma((8,)), dma((2, 9)), dma((2, 6)), dma((2, 6)), dma((2, 4)), dma((2, 4)), dma((2, 7)), dma((2, 7)),
                 dma((9,)), dma((9,)), dma((2, n_loc)), dma((2, n_loc)), dma((2, 6)), dma((2, 6)), dma((2,)),
                 pltpu.SemaphoreType.REGULAR,
             ],
             compiler_params=pltpu.CompilerParams(collective_id=0, has_side_effects=True, vmem_limit_bytes=67043328),
-        )(meta, tokens_a, tokens_b, shared_w1, shared_w3, shared_w2, routed_w1, routed_w3, routed_w2)
-        return outs[0], outs[1]
+        )(*routing, tokens_a, tokens_b, shared_w1, shared_w3, shared_w2, routed_w1, routed_w3, routed_w2)
+        return pl.pallas_call(
+            place_kernel,
+            out_shape=(jax.ShapeDtypeStruct((rows, width), bf),) * 2,
+            in_specs=[any_spec] * 2,
+            out_specs=[any_spec] * 2,
+            scratch_shapes=[pltpu.VMEM((2, rows, width), bf), dma((2,)), dma((2,))],
+        )(outs[0], outs[1])
 
     return jax.shard_map(layer_local, mesh=mesh, in_specs=in_specs, out_specs=(tok_spec, tok_spec), check_vma=False)

time: 183 us -> 171 us (0.934)
  local copies, waits for them, and re-layouts: 4.13 us -> 0 us
  Pallas kernels: 174 us -> 170 us
  other arithmetic: 3.5 us -> 0 us
    pallas_call x1, Pallas kernels: 174 us -> 168 us  [layer_local(): pl.pallas_call(functools.partial(layer_kernel, (top_k, ep_size, tp_size,...]
    unnamed x2 -> x0, local copies, waits for them, and re-layouts: 4.13 us -> none
    transpose x4 -> x0, other arithmetic: 2.88 us -> none  [the longest x2 1.44 us: routing_rows(): ids = jnp.where(keep, expert_ids * cap + slot_ids, -1).astype(jnp.float32).T]
    pallas_call x0 -> x1, Pallas kernels: none -> 2.31 us  [layer_local(): pl.pallas_call(place_kernel, out_shape=(jax.ShapeDtypeStruct((rows, width...]
where the time goes in v2:
time: 171 us
  Pallas kernels  170 us (99%)
    pallas_call x1, Pallas kernels, layer_local(): pl.pallas_call(functools.partial(layer_kernel, (top_k, ep_size, tp_size,...  168 us

profile of v2, /device:TPU:97, one launch (start us, length us, event | category | flops | bytes accessed | tf_op | source)
XLA Modules:
  0.0 170.7 jit_solution(6760864661854275682)
XLA Ops:
  0.6 167.7 %shard_map.149 = (bf16[256,1536]{1,0:T(8,128)(2,1)}, bf16[256,1536]{1,0:T(8,128)(2,1)}, bf16[3,1536,256]{2,1,0:T(8,128)(2,1)}, bf16[3,1536,256]{2,1,0:T(8,128)(2,1)}, bf16[3,256,1536]{2,1,0:T(8,128)(2,1)}) custom-call(s32[6,256]{1,0:T(8,128)} %bitcast.6, s32[6,256]{1,0:T(8,128)} %bitcast.7, f32[6,256]{1,0:T(8,128)} %bitcast.8, f32[6,256]{1,0:T(8,128)} %bitcast.9, ...), custom_call_target="tpu_custom_call" | custom-call | tf_op jit(solution)/shard_map/pallas_call | solution.py:364
  168.4 2.3 %shard_map.150 = (bf16[256,1536]{1,0:T(8,128)(2,1)}, bf16[256,1536]{1,0:T(8,128)(2,1)}) custom-call(bf16[256,1536]{1,0:T(8,128)(2,1)} %get-tuple-element.4.a, bf16[256,1536]{1,0:T(8,128)(2,1)} %get-tuple-element.5.b), custom_call_target="tpu_custom_call" | custom-call | tf_op jit(solution)/shard_map/pallas_call | solution.py:389

commit v3 on v2

v3 whole, which is shorter than its diff:
```python
import functools

import jax
import jax.numpy as jnp
from jax import lax
from jax.experimental import pallas as pl
from jax.experimental.pallas import tpu as pltpu
from jax.sharding import PartitionSpec as P

MESH = pl.DeviceIdType.MESH
VMEM_BYTES = 65000000
CORES = 2
OWN, NEXT, PREV, FAR = 0, 1, 2, 3


def capacity_rows(tok_local, top_k, num_experts):
    return max(4, (2 * tok_local * top_k) // num_experts)


def split_three(value):
    hi = value.astype(jnp.bfloat16)
    rest = value - hi.astype(jnp.float32)
    mid = rest.astype(jnp.bfloat16)
    low = (rest - mid.astype(jnp.float32)).astype(jnp.bfloat16)
    return hi, mid, low


def layer_kernel(cfg, ea, eb, ga, gb, sa, sb, ta, tb, s1, s3, s2, w1, w3, w2, out_a, out_b, g1, g3, g2,
                 tok, routing, stage_e, stage_s, stage_g, xr, rp, w1b, w3b, w2b, part, rs1, rfull,
                 loc_sem, w_sem, tx_send, tx_recv, tp_send, tp_recv, mt_send, mt_recv,
                 y_send, y_recv, r_send, r_recv, c_send, c_recv, free_sem, y_ready):
    top_k, ep_size, tp_size, cap = cfg
    n_loc = w1.shape[0]
    ff = w1.shape[2]
    sh = s1.shape[1]
    rows, width = ta.shape
    half = rows // 2
    exp_rows = n_loc * cap
    nx = ep_size // CORES
    ep = lax.axis_index('ep')
    ty = lax.axis_index('tp')
    core = ep % CORES
    chip = ep // CORES
    partner = chip * CORES + (1 - core)
    x_next = ((chip + 1) % nx) * CORES + core
    x_prev = ((chip + nx - 1) % nx) * CORES + core
    y_next = (ty + 1) % tp_size
    y_prev = (ty + tp_size - 1) % tp_size
    to_xn, to_xp, to_pr = {'ep': x_next}, {'ep': x_prev}, {'ep': partner}
    to_yn, to_yp = {'tp': y_next}, {'tp': y_prev}
    lo, hi = pl.ds(0, half), pl.ds(half, half)

    def remote(src, dst, ssem, rsem, dev):
        return pltpu.make_async_remote_copy(src_ref=src, dst_ref=dst, send_sem=ssem, recv_sem=rsem,
                                            device_id=dev, device_id_type=MESH)

    def own_sends(m):
        mine = (ta, tb)[m]
        return [remote(mine.at[lo], tok.at[m, PREV, lo], tx_send.at[m, 0], tx_recv.at[m, 0], to_xn),
                remote(mine.at[hi], tok.at[m, NEXT, hi], tx_send.at[m, 3], tx_recv.at[m, 3], to_xp),
                remote(mine.at[hi], tok.at[m, PREV, hi], tx_send.at[m, 1], tx_recv.at[m, 1], to_xn),
                remote(mine.at[lo], tok.at[m, NEXT, lo], tx_send.at[m, 2], tx_recv.at[m, 2], to_xp)]

    def forwards(m):
        return [remote(tok.at[m, PREV, lo], tok.at[m, FAR, lo], tx_send.at[m, 4], tx_recv.at[m, 4], to_xn),
                remote(tok.at[m, NEXT, hi], tok.at[m, FAR, hi], tx_send.at[m, 5], tx_recv.at[m, 5], to_xp)]

    def to_partner(m, k):
        return remote((ta, tb)[m] if k == OWN else tok.at[m, k], tok.at[m, k + 4], tp_send.at[m, k], tp_recv.at[m, k], to_pr)

    def meta(i, src, dst, dev, lines=pl.ds(0, 4 * top_k)):
        return remote(routing.at[src, lines], routing.at[dst, lines], mt_send.at[i], mt_recv.at[i], dev)

    far_cut = (4 * top_k * 2 // 3) // 8 * 8
    meta_next = meta(0, OWN, PREV, to_xn)
    meta_prev = meta(1, OWN, NEXT, to_xp)
    meta_far = [meta(2, PREV, FAR, to_xn, pl.ds(0, far_cut)),
                meta(3, NEXT, FAR, to_xp, pl.ds(far_cut, 4 * top_k - far_cut))]
    meta_pair = [meta(4 + k, k, k + 4, to_pr) for k in range(4)]
    y_own = []
    for i, (src, dst) in enumerate(((s1, g1), (s2, g2), (s3, g3))):
        y_own.append(remote(src, dst.at[PREV - 1], y_send.at[i], y_recv.at[i], to_yn))
        y_own.append(remote(src, dst.at[NEXT - 1], y_send.at[3 + i], y_recv.at[3 + i], to_yp))
    y_far = [remote(g1.at[PREV - 1], g1.at[FAR - 1], y_send.at[6], y_recv.at[6], to_yn),
             remote(g2.at[PREV - 1], g2.at[FAR - 1], y_send.at[7], y_recv.at[7], to_yn),
             remote(g3.at[NEXT - 1], g3.at[FAR - 1], y_send.at[8], y_recv.at[8], to_yp)]

    def weights(e, slot):
        return [pltpu.make_async_copy(w1.at[e], w1b.at[slot], w_sem.at[slot, 0]),
                pltpu.make_async_copy(w3.at[e], w3b.at[slot], w_sem.at[slot, 1]),
                pltpu.make_async_copy(w2.at[e], w2b.at[slot], w_sem.at[slot, 2])]

    def push_rows(m, e):
        return remote(xr.at[e, pl.ds(4, 4)], rp.at[e], r_send.at[m, e], r_recv.at[m, e], to_pr)

    def first_far(m):
        return [remote(part.at[m, FAR, hi], rs1.at[m, 0], c_send.at[m, 4], c_recv.at[m, 4], to_xn),
                remote(part.at[m, FAR, lo], rs1.at[m, 1], c_send.at[m, 5], c_recv.at[m, 5], to_xp)]

    def near_own(m):
        return [remote(part.at[m, NEXT, lo], rfull.at[m, 0, lo], c_send.at[m, 0], c_recv.at[m, 0], to_xn),
                remote(part.at[m, PREV, hi], rfull.at[m, 1, hi], c_send.at[m, 1], c_recv.at[m, 1], to_xp)]

    def near_sum(m):
        return [remote(part.at[m, NEXT, hi], rfull.at[m, 0, hi], c_send.at[m, 2], c_recv.at[m, 2], to_xn),
                remote(part.at[m, PREV, lo], rfull.at[m, 1, lo], c_send.at[m, 3], c_recv.at[m, 3], to_xp)]

    tables = [pltpu.make_async_copy(src, dst, loc_sem.at[i]) for i, (src, dst) in enumerate((
        (ea, stage_e.at[0]), (sa, stage_s.at[0]), (ga, stage_g.at[0]),
        (eb, stage_e.at[1]), (sb, stage_s.at[1]), (gb, stage_g.at[1])))]
    local = [pltpu.make_async_copy(ta, tok.at[0, OWN], loc_sem.at[6]),
             pltpu.make_async_copy(tb, tok.at[1, OWN], loc_sem.at[7])]
    barrier = pltpu.get_barrier_semaphore()
    even_row = ty % 2 == 0
    for dev in (to_xn, to_xp, to_pr):
        pl.semaphore_signal(barrier, inc=1, device_id=dev, device_id_type=MESH)
    for cp in tables + local:
        cp.start()

    @pl.when(even_row)
    def _():
        pl.semaphore_wait(barrier, 3)
        for dev in (to_yn, to_yp):
            pl.semaphore_signal(barrier, inc=1, device_id=dev, device_id_type=MESH)

    @pl.when(jnp.logical_not(even_row))
    def _():
        pl.semaphore_wait(barrier, 5)
        for dev in (to_yn, to_yp):
            pl.semaphore_signal(y_ready, inc=1, device_id=dev, device_id_type=MESH)
    first = own_sends(0)
    for cp in first[:2] + [to_partner(0, OWN)]:
        cp.start()
    for cp in tables:
        cp.wait()
    for m in range(2):
        kept = stage_s[m] >= 0
        ids = jnp.where(kept, stage_e[m] * cap + stage_s[m], -1).astype(jnp.float32)
        routing[OWN, pl.ds(2 * m * top_k, top_k)] = ids
        routing[OWN, pl.ds((2 * m + 1) * top_k, top_k)] = jnp.where(kept, stage_g[m], 0.0)
    for cp in weights(0, 0) + [meta_next, meta_prev, meta_pair[OWN]] + first[2:]:
        cp.start()
    for cp in local:
        cp.wait()

    row_id = lax.broadcasted_iota(jnp.int32, (exp_rows, rows), 0).astype(jnp.float32)

    def placed(ids, base, values):
        shifted = row_id + (base * exp_rows).astype(jnp.float32)
        total = jnp.zeros((exp_rows, rows), jnp.float32)
        for j in range(top_k):
            total = jnp.where(shifted == ids[j:j + 1, :], 1.0 if values is None else values[j:j + 1, :], total)
        return total

    def row_ids(k, m):
        return routing[k, pl.ds(2 * m * top_k, top_k), :]

    def gates(k, m):
        return routing[k, pl.ds((2 * m + 1) * top_k, top_k), :]

    def pass_tokens():
        first[0].wait_recv()
        first[1].wait_recv()
        for cp in (meta_next, meta_prev):
            cp.wait_recv()
        for cp in forwards(0) + meta_far + own_sends(1) + [meta_pair[NEXT], meta_pair[PREV], to_partner(1, OWN)]:
            cp.start()

        @pl.when(even_row)
        def _():
            pl.semaphore_wait(y_ready, 2)
        for cp in y_own:
            cp.start()

    def arrivals(step):
        if step == 1:
            for cp in (meta_pair[OWN], to_partner(0, OWN)):
                cp.wait_recv()
        elif step == 2:
            first[2].wait_recv()
            first[3].wait_recv()
            to_partner(0, NEXT).start()
            to_partner(0, PREV).start()
        elif step in (3, 5):
            k = NEXT if step == 3 else PREV
            for cp in (meta_pair[k], to_partner(0, k)):
                cp.wait_recv()
        elif step == 6:
            for cp in meta_far:
                cp.wait_recv()
            meta_pair[FAR].start()
            for cp in forwards(0):
                cp.wait_recv()
            to_partner(0, FAR).start()
        elif step == 7:
            for cp in (meta_pair[FAR], to_partner(0, FAR)):
                cp.wait_recv()

    def pair_slot(block):
        return (block + 2) % 3 + block // 3

    def gather(m, first_step, last_step):
        def one(step, carry):
            if m == 0:
                for at in range(max(first_step, 1), last_step):
                    if at == 6:
                        continue
                    pl.when(step == at)(functools.partial(arrivals, at))
            block, other = step // 2, step % 2
            k = other * 4 + block
            place = placed(row_ids(k, m), ep, None).astype(jnp.bfloat16)
            got = jnp.dot(place, tok[m, k], preferred_element_type=jnp.float32).astype(jnp.bfloat16)
            at = (1 - other) * ((block + 1) % 4) + other * (4 + pair_slot(block))
            xr[:, at] = got.reshape(n_loc, cap, width)
            return carry
        lax.fori_loop(first_step, last_step, one, 0)

    def swiglu(x_rows, slot):
        proj_in = jnp.dot(x_rows, w1b[slot], preferred_element_type=jnp.float32)
        proj_gate = jnp.dot(x_rows, w3b[slot], preferred_element_type=jnp.float32)
        hidden = (jax.nn.silu(proj_in) * proj_gate).astype(jnp.bfloat16)
        return jnp.dot(hidden, w2b[slot], preferred_element_type=jnp.float32)

    def second_arrivals(step):
        sends = own_sends(1)
        if step == 0:
            sends[0].wait_recv()
            sends[1].wait_recv()
            for cp in forwards(1):
                cp.start()
        else:
            sends[2].wait_recv()
            sends[3].wait_recv()
            to_partner(1, NEXT).start()
            to_partner(1, PREV).start()

    early = n_loc // 2

    def run(e, slot, blocks):
        total = sum(b.size for b in blocks)
        x_rows = jnp.concatenate([xr[e, b].reshape(b.size * cap, width) for b in blocks], axis=0)
        res = swiglu(x_rows, slot).astype(jnp.bfloat16).reshape(total, cap, width)
        at = 0
        for b in blocks:
            xr[e, b] = res[at:at + b.size]
            at += b.size

    def stream(first, last, following, blocks, push, events=()):
        def one(e, carry):
            slot = e % 2
            for cp in weights(following(e), 1 - slot):
                cp.start()
            if push:
                @pl.when(e > 0)
                def _():
                    push_rows(0, e - 1).start()
            for cp in weights(e, slot):
                cp.wait()
            run(e, slot, blocks)
            for at, event in events:
                pl.when(e == at)(event)
            return carry
        lax.fori_loop(first, last, one, 0)

    def experts_first():
        own, far = [pl.ds(1, 1), pl.ds(6, 1)], [pl.ds(0, 1), pl.ds(7, 1)]
        near = [pl.ds(2, 4)]
        gather(0, 0, 2)
        stream(0, n_loc, lambda e: (e + 1) % n_loc, own, False, [(n_loc - 3, pass_tokens)])
        gather(0, 2, 6)
        stream(0, early, lambda e: (e + 1) % early, near, False, [(early - 2, functools.partial(arrivals, 6))])
        gather(0, 6, 8)
        stream(0, early, lambda e: e + 1, far, True, [(early - 1, functools.partial(second_arrivals, 0))])
        stream(early, n_loc, lambda e: (e + 1) % n_loc, [far[0]] + near + [far[1]], True)
        push_rows(0, n_loc - 1).start()

    def experts_second():
        def one(e, carry):
            slot = e % 2

            @pl.when(e < n_loc - 1)
            def _():
                for cp in weights(e + 1, 1 - slot):
                    cp.start()

            @pl.when(e > 0)
            def _():
                push_rows(1, e - 1).start()
            for cp in weights(e, slot):
                cp.wait()
            run(e, slot, [pl.ds(0, 8)])

            @pl.when(e == early)
            def _():
                for cp in y_own:
                    cp.wait_recv()
                for cp in y_far:
                    cp.start()
            return carry
        lax.fori_loop(0, n_loc, one, 0)
        push_rows(1, n_loc - 1).start()

    def combine(m):
        chunks = [pl.ds(n * 256, 256) for n in range(width // 256)]

        def weigh(gate_rows, rows_of, cols):
            acc = jnp.dot(gate_rows, rows_of(cols).reshape(exp_rows, 256), preferred_element_type=jnp.float32)
            return acc[0:rows] + acc[rows:2 * rows] + acc[2 * rows:3 * rows]

        def one(step, carry):
            i = 3 - step
            ids = row_ids(i, m)
            vals = gates(i, m)
            mine = jnp.concatenate(split_three(placed(ids, ep, vals).T), axis=0)
            other = jnp.concatenate(split_three(placed(ids, partner, vals).T), axis=0)
            at = (i + 1) % 4
            for cols in chunks:
                part[m, i, :, cols] = weigh(mine, lambda c: xr[:, at, :, c], cols)

            @pl.when(step == 0)
            def _():
                for e in range(n_loc):
                    push_rows(m, e).wait_recv()
            for cols in chunks:
                part[m, i, :, cols] += weigh(other, lambda c: rp[:, pair_slot(i), :, c], cols)

            @pl.when(step == 0)
            def _():
                for cp in first_far(m):
                    cp.start()

            @pl.when(step == 1)
            def _():
                near_own(m)[1].start()
                if m == 0:
                    second_arrivals(1)

            @pl.when(step == 2)
            def _():
                near_own(m)[0].start()
            return carry
        lax.fori_loop(0, 4, one, 0)

    def pass_on(m):
        incoming = first_far(m)
        sends = near_sum(m)
        incoming[0].wait_recv()
        part[m, NEXT, hi] = part[m, NEXT, hi] + rs1[m, 0]
        sends[0].start()
        incoming[1].wait_recv()
        part[m, PREV, lo] = part[m, PREV, lo] + rs1[m, 1]
        sends[1].start()

    def finish(m, out):
        for cp in near_own(m) + near_sum(m):
            cp.wait_recv()
        total = part[m, OWN] + tok[m, OWN].astype(jnp.float32) + rfull[m, 0] + rfull[m, 1]
        out[...] = total.astype(jnp.bfloat16)

    experts_first()
    combine(0)
    for cp in forwards(1):
        cp.wait_recv()
    to_partner(1, FAR).start()
    pl.semaphore_signal(free_sem, inc=1, device_id=to_pr, device_id_type=MESH)
    for k in range(4):
        to_partner(1, k).wait_recv()
    for e in range(n_loc):
        push_rows(0, e).wait_send()
    gather(1, 0, 8)
    pl.semaphore_wait(free_sem, 1)
    experts_second()
    pass_on(0)
    combine(1)
    for cp in y_far:
        cp.wait_recv()
    shared = []
    for slot, pair in enumerate((((s1, s3, s2), NEXT), (None, FAR))):
        srcs = [pair[0] or (g1.at[PREV - 1], g3.at[PREV - 1], g2.at[PREV - 1]), (g1.at[pair[1] - 1], g3.at[pair[1] - 1], g2.at[pair[1] - 1])]
        for p, (a1, a3, a2) in enumerate(srcs):
            part_of = pl.ds(p * sh, sh)
            shared.append(pltpu.make_async_copy(a1, w1b.at[slot, :, part_of], w_sem.at[slot, 3 + p]))
            shared.append(pltpu.make_async_copy(a3, w3b.at[slot, :, part_of], w_sem.at[slot, 5 + p]))
            shared.append(pltpu.make_async_copy(a2, w2b.at[slot, part_of, :], w_sem.at[slot, 7 + p]))
    for cp in shared:
        cp.start()
    for cp in shared:
        cp.wait()

    def shared_one(i, carry):
        m = i // 2
        part[m, OWN] = part[m, OWN] + swiglu(tok[m, OWN], i % 2)
        return carry
    lax.fori_loop(0, 4, shared_one, 0)

    finish(0, out_a)
    pass_on(1)
    finish(1, out_b)
    for m in range(2):
        for k in range(4):
            to_partner(m, k).wait_send()
        for cp in own_sends(m) + forwards(m) + first_far(m) + near_own(m) + near_sum(m):
            cp.wait_send()
    for e in range(n_loc):
        push_rows(1, e).wait_send()
    for cp in [meta_next, meta_prev] + meta_far + meta_pair + y_own + y_far:
        cp.wait_send()


def solution(mesh):
    ep_size = mesh.shape['ep']
    tp_size = mesh.shape['tp']
    tok_spec = P(('data', 'ep', 'tp'), None)
    in_specs = (tok_spec,) * 8 + (P(None, 'tp'), P(None, 'tp'), P('tp', None), P('ep', None, None), P('ep', None, None), P('ep', None, None))

    def layer_local(tokens_a, tokens_b, experts_a, experts_b, gates_a, gates_b, slots_a, slots_b, shared_w1, shared_w3, shared_w2, routed_w1, routed_w3, routed_w2):
        rows, width = tokens_a.shape
        top_k = experts_a.shape[1]
        n_loc, _, ff = routed_w1.shape
        sh = shared_w1.shape[1]
        cap = capacity_rows(rows, top_k, n_loc * ep_size)
        half = rows // 2
        tables = [a.T for a in (experts_a, experts_b, gates_a, gates_b, slots_a, slots_b)]
        bf, f32 = jnp.bfloat16, jnp.float32
        dma = pltpu.SemaphoreType.DMA
        any_spec = pl.BlockSpec(memory_space=pl.ANY)
        vmem_spec = pl.BlockSpec(memory_space=pltpu.VMEM)
        outs = pl.pallas_call(
            functools.partial(layer_kernel, (top_k, ep_size, tp_size, cap)),
            out_shape=(pltpu.VMEM((rows, width), bf), pltpu.VMEM((rows, width), bf),
                       jax.ShapeDtypeStruct((3, width, sh), bf), jax.ShapeDtypeStruct((3, width, sh), bf),
                       jax.ShapeDtypeStruct((3, sh, width), bf)),
            in_specs=[any_spec] * 14,
            out_specs=[vmem_spec] * 2 + [any_spec] * 3,
            scratch_shapes=[
                pltpu.VMEM((2, 8, rows, width), bf),
                pltpu.VMEM((8, 4 * top_k, rows), f32),
                pltpu.VMEM((2, top_k, rows), jnp.int32),
                pltpu.VMEM((2, top_k, rows), jnp.int32),
                pltpu.VMEM((2, top_k, rows), f32),
                pltpu.VMEM((n_loc, 8, cap, width), bf),
                pltpu.VMEM((n_loc, 4, cap, width), bf),
                pltpu.VMEM((2, width, ff), bf),
                pltpu.VMEM((2, width, ff), bf),
                pltpu.VMEM((2, ff, width), bf),
                pltpu.VMEM((2, 4, rows, width), f32),
                pltpu.VMEM((2, 2, half, width), f32),
                pltpu.VMEM((2, 2, rows, width), f32),
                dma((8,)), dma((2, 9)), dma((2, 6)), dma((2, 6)), dma((2, 4)), dma((2, 4)), dma((8,)), dma((8,)),
                dma((9,)), dma((9,)), dma((2, n_loc)), dma((2, n_loc)), dma((2, 6)), dma((2, 6)),
                pltpu.SemaphoreType.REGULAR, pltpu.SemaphoreType.REGULAR,
            ],
            compiler_params=pltpu.CompilerParams(collective_id=0, has_side_effects=True, vmem_limit_bytes=VMEM_BYTES),
        )(*tables, tokens_a, tokens_b, shared_w1, shared_w3, shared_w2, routed_w1, routed_w3, routed_w2)
        return outs[0], outs[1]

    return jax.shard_map(layer_local, mesh=mesh, in_specs=in_specs, out_specs=(tok_spec, tok_spec), check_vma=False)
```

time: 171 us -> 164 us (0.959); the launches traced: 171 us -> 162 us
  Pallas kernels: 170 us -> 159 us
  local copies, waits for them, and re-layouts: 0 us -> 1.76 us
    pallas_call x1, Pallas kernels: 168 us -> 159 us  [layer_local(): pl.pallas_call(functools.partial(layer_kernel, (top_k, ep_size, tp_size,...]
    pallas_call x1 -> x0, Pallas kernels: 2.31 us -> none  [layer_local(): pl.pallas_call(place_kernel, out_shape=(jax.ShapeDtypeStruct((rows, width...]
    unnamed x0 -> x2, local copies, waits for them, and re-layouts: none -> 1.76 us
where the time goes in v3:
time: 164 us; the launch traced here: 162 us
  Pallas kernels  159 us (97%)
  local copies, waits for them, and re-layouts  1.76 us (1%)
    pallas_call x1, Pallas kernels, layer_local(): pl.pallas_call(functools.partial(layer_kernel, (top_k, ep_size, tp_size,...  159 us

profile of v3, /device:TPU:97, one launch (start us, length us, event | category | flops | bytes accessed | tf_op | source)
XLA Modules:
  0.0 161.8 jit_solution(16393410436319377677)
XLA Ops:
  0.6 159.3 %shard_map.149 = (bf16[256,1536]{1,0:T(8,128)(2,1)S(1)}, bf16[256,1536]{1,0:T(8,128)(2,1)S(1)}, bf16[3,1536,256]{2,1,0:T(8,128)(2,1)}, bf16[3,1536,256]{2,1,0:T(8,128)(2,1)}, bf16[3,256,1536]{2,1,0:T(8,128)(2,1)}) custom-call(s32[6,256]{1,0:T(8,128)} %bitcast.6, s32[6,256]{1,0:T(8,128)} %bitcast.7, f32[6,256]{1,0:T(8,128)} %bitcast.8, f32[6,256]{1,0:T(8,128)} %bitcast.9, ...), custom_call_target="tpu_custom_call" | custom-call | tf_op jit(solution)/shard_map/pallas_call | solution.py:428
  160.0 0.9 copy.18
  160.9 0.9 copy.19

commit v4 on v3

--- a/solution.py
+++ b/solution.py
@@ -111,23 +111,33 @@
     local = [pltpu.make_async_copy(ta, tok.at[0, OWN], loc_sem.at[6]),
              pltpu.make_async_copy(tb, tok.at[1, OWN], loc_sem.at[7])]
     barrier = pltpu.get_barrier_semaphore()
-    even_row = ty % 2 == 0
+    is_first, is_last = ty == 0, ty == tp_size - 1
+
+    def greet(sem, dev):
+        pl.semaphore_signal(sem, inc=1, device_id=dev, device_id_type=MESH)
+
     for dev in (to_xn, to_xp, to_pr):
-        pl.semaphore_signal(barrier, inc=1, device_id=dev, device_id_type=MESH)
+        greet(barrier, dev)
     for cp in tables + local:
         cp.start()
 
-    @pl.when(even_row)
+    @pl.when(is_first)
     def _():
         pl.semaphore_wait(barrier, 3)
-        for dev in (to_yn, to_yp):
-            pl.semaphore_signal(barrier, inc=1, device_id=dev, device_id_type=MESH)
-
-    @pl.when(jnp.logical_not(even_row))
+        greet(barrier, to_yn)
+        greet(barrier, to_yp)
+
+    @pl.when(jnp.logical_not(jnp.logical_or(is_first, is_last)))
+    def _():
+        pl.semaphore_wait(barrier, 4)
+        greet(barrier, to_yn)
+        greet(y_ready, to_yp)
+
+    @pl.when(is_last)
     def _():
         pl.semaphore_wait(barrier, 5)
-        for dev in (to_yn, to_yp):
-            pl.semaphore_signal(y_ready, inc=1, device_id=dev, device_id_type=MESH)
+        greet(y_ready, to_yn)
+        greet(y_ready, to_yp)
     first = own_sends(0)
     for cp in first[:2] + [to_partner(0, OWN)]:
         cp.start()
@@ -166,9 +176,13 @@
         for cp in forwards(0) + meta_far + own_sends(1) + [meta_pair[NEXT], meta_pair[PREV], to_partner(1, OWN)]:
             cp.start()
 
-        @pl.when(even_row)
+        @pl.when(is_first)
         def _():
             pl.semaphore_wait(y_ready, 2)
+
+        @pl.when(jnp.logical_not(jnp.logical_or(is_first, is_last)))
+        def _():
+            pl.semaphore_wait(y_ready, 1)
         for cp in y_own:
             cp.start()
 
@@ -351,11 +365,18 @@
         part[m, PREV, lo] = part[m, PREV, lo] + rs1[m, 1]
         sends[1].start()
 
+    def near_ready(m):
+        for cp in near_own(m):
+            cp.wait_recv()
+        part[m, OWN, lo] += tok[m, OWN, lo].astype(jnp.float32) + rfull[m, 0, lo]
+        part[m, OWN, hi] += tok[m, OWN, hi].astype(jnp.float32) + rfull[m, 1, hi]
+
     def finish(m, out):
-        for cp in near_own(m) + near_sum(m):
-            cp.wait_recv()
-        total = part[m, OWN] + tok[m, OWN].astype(jnp.float32) + rfull[m, 0] + rfull[m, 1]
-        out[...] = total.astype(jnp.bfloat16)
+        sums = near_sum(m)
+        sums[0].wait_recv()
+        out[hi] = (part[m, OWN, hi] + rfull[m, 0, hi]).astype(jnp.bfloat16)
+        sums[1].wait_recv()
+        out[lo] = (part[m, OWN, lo] + rfull[m, 1, lo]).astype(jnp.bfloat16)
 
     experts_first()
     combine(0)
@@ -393,8 +414,10 @@
         return carry
     lax.fori_loop(0, 4, shared_one, 0)
 
+    near_ready(0)
     finish(0, out_a)
     pass_on(1)
+    near_ready(1)
     finish(1, out_b)
     for m in range(2):
         for k in range(4):
@@ -405,6 +428,14 @@
         push_rows(1, e).wait_send()
     for cp in [meta_next, meta_prev] + meta_far + meta_pair + y_own + y_far:
         cp.wait_send()
+
+
+def place_kernel(a, b, out_a, out_b, sem):
+    copies = [pltpu.make_async_copy(a, out_a, sem.at[0]), pltpu.make_async_copy(b, out_b, sem.at[1])]
+    for cp in copies:
+        cp.start()
+    for cp in copies:
+        cp.wait()
 
 
 def solution(mesh):
@@ -452,6 +483,14 @@
             ],
             compiler_params=pltpu.CompilerParams(collective_id=0, has_side_effects=True, vmem_limit_bytes=VMEM_BYTES),
         )(*tables, tokens_a, tokens_b, shared_w1, shared_w3, shared_w2, routed_w1, routed_w3, routed_w2)
-        return outs[0], outs[1]
+        held = outs[:2]
+        return pl.pallas_call(
+            place_kernel,
+            out_shape=(jax.ShapeDtypeStruct((rows, width), bf),) * 2,
+            in_specs=[vmem_spec] * 2,
+            out_specs=[any_spec] * 2,
+            scratch_shapes=[dma((2,))],
+            compiler_params=pltpu.CompilerParams(vmem_limit_bytes=1 << 20),
+        )(*held)
 
     return jax.shard_map(layer_local, mesh=mesh, in_specs=in_specs, out_specs=(tok_spec, tok_spec), check_vma=False)

time: 164 us -> 161 us (0.982); the launches traced: 162 us -> 161 us
  local copies, waits for them, and re-layouts: 1.76 us -> 0 us
    unnamed x2 -> x0, local copies, waits for them, and re-layouts: 1.76 us -> none
where the time goes in v4:
time: 161 us
  Pallas kernels  160 us (99%)
    pallas_call x1, Pallas kernels, layer_local(): pl.pallas_call(functools.partial(layer_kernel, (top_k, ep_size, tp_size,...  159 us

profile of v4, /device:TPU:97, one launch (start us, length us, event | category | flops | bytes accessed | tf_op | source)
XLA Modules:
  0.0 161.0 jit_solution(10756359595348187092)
XLA Ops:
  0.6 159.2 %shard_map.149 = (bf16[256,1536]{1,0:T(8,128)(2,1)S(1)}, bf16[256,1536]{1,0:T(8,128)(2,1)S(1)}, bf16[3,1536,256]{2,1,0:T(8,128)(2,1)}, bf16[3,1536,256]{2,1,0:T(8,128)(2,1)}, bf16[3,256,1536]{2,1,0:T(8,128)(2,1)}) custom-call(s32[6,256]{1,0:T(8,128)} %bitcast.6, s32[6,256]{1,0:T(8,128)} %bitcast.7, f32[6,256]{1,0:T(8,128)} %bitcast.8, f32[6,256]{1,0:T(8,128)} %bitcast.9, ...), custom_call_target="tpu_custom_call" | custom-call | tf_op jit(solution)/shard_map/pallas_call | solution.py:459
  159.9 1.2 shard_map.150

commit v5 on v4

--- a/solution.py
+++ b/solution.py
@@ -9,6 +9,7 @@
 
 MESH = pl.DeviceIdType.MESH
 VMEM_BYTES = 65000000
+BF16_TOP = float(jnp.finfo(jnp.bfloat16).max)
 CORES = 2
 OWN, NEXT, PREV, FAR = 0, 1, 2, 3
 
@@ -18,7 +19,7 @@
 
 
 def split_three(value):
-    hi = value.astype(jnp.bfloat16)
+    hi = jnp.minimum(value, BF16_TOP).astype(jnp.bfloat16)
     rest = value - hi.astype(jnp.float32)
     mid = rest.astype(jnp.bfloat16)
     low = (rest - mid.astype(jnp.float32)).astype(jnp.bfloat16)

time: 161 us -> 161 us (level)
  no operation moved by 1% of the time
where the time goes in v5:
time: 161 us
  Pallas kernels  160 us (99%)
    pallas_call x1, Pallas kernels, layer_local(): pl.pallas_call(functools.partial(layer_kernel, (top_k, ep_size, tp_size,...  159 us

profile of v5, /device:TPU:97, one launch (start us, length us, event | category | flops | bytes accessed | tf_op | source)
XLA Modules:
  0.0 161.0 jit_solution(1269423366981456405)
XLA Ops:
  0.6 159.2 %shard_map.149 = (bf16[256,1536]{1,0:T(8,128)(2,1)S(1)}, bf16[256,1536]{1,0:T(8,128)(2,1)S(1)}, bf16[3,1536,256]{2,1,0:T(8,128)(2,1)}, bf16[3,1536,256]{2,1,0:T(8,128)(2,1)}, bf16[3,256,1536]{2,1,0:T(8,128)(2,1)}) custom-call(s32[6,256]{1,0:T(8,128)} %bitcast.6, s32[6,256]{1,0:T(8,128)} %bitcast.7, f32[6,256]{1,0:T(8,128)} %bitcast.8, f32[6,256]{1,0:T(8,128)} %bitcast.9, ...), custom_call_target="tpu_custom_call" | custom-call | tf_op jit(solution)/shard_map/pallas_call | solution.py:460
  159.9 1.2 shard_map.150
